TPU v7x, 32 devices: a whole 2x2x4 slice. The times are simulated.
32 devices in a mesh: expert: 16 (over z, y, core), dp: 2 (over x).
Axes of the slice: x: 2, y: 2, z: 4, core: 2. Of those that a mesh axis runs over, the one named last changes fastest.
Arguments:
- tokens: bfloat16 [4096, 7168], P(('expert', 'dp')), may hold values from -6 to 6
- cotangent: bfloat16 [4096, 7168], P(('expert', 'dp')), may hold values from -1.5 to 1.5
- routes: int32 [4096, 8], P(('expert', 'dp')), may hold values from 0 to 255, all different within a row; in each aligned block of 128 rows (0 to 127, 128 to 255, ...) at most 9 rows name the same one
- route_gates: float32 [4096, 8], P(('expert', 'dp')), may hold values from 0.1 to 1
- gate_weight: bfloat16 [16, 7168, 256], P('expert'), may hold values from -0.0625 to 0.0625
- up_weight: bfloat16 [16, 7168, 256], P('expert'), may hold values from -0.0625 to 0.0625
- down_weight: bfloat16 [16, 256, 7168], P('expert'), may hold values from -0.125 to 0.125
Outputs:
- grad_gate: bfloat16 [16, 7168, 256], P('expert')
- grad_up: bfloat16 [16, 7168, 256], P('expert')
- grad_down: bfloat16 [16, 256, 7168], P('expert')
Inputs may be any that keep to these rules, and one draw needn't show every extreme that they name: `routes`: each row names 8 different experts; among the rows of one device no expert is named more than 9 times.
All inputs are finite; a program needn't handle non-finite values.
Results may differ from a plain program's by a relative error of at most 0.0065.
Values may be sent and summed in bfloat16 or wider, within the bound.
No kernel may reach another device: no remote copies, remote signals or barrier semaphores. Data moves between devices by JAX's collectives and lax.ppermute only.
A program may use at most 192 MiB of HBM per device.

v0:
```python
import functools

import jax
import jax.numpy as jnp
from jax import lax
from jax.experimental import pallas as pl
from jax.experimental.pallas import tpu as pltpu
from jax.sharding import PartitionSpec as P


HIDDEN_SIZE = 2048
CAP = 9
LANES = 128
SUBLANES = 8
AXES = ("expert", "dp")
KERNEL_VMEM = 28 * 1024 * 1024
PIECE = 1280


def hop(block, even, odd=None):
    experts = lax.axis_size("expert")
    replicas = lax.axis_size("dp")
    route = []
    for e in range(experts):
        flip, turn = even if odd is None or e % 2 == 0 else odd
        for r in range(replicas):
            route.append((e * replicas + r, (e ^ flip) * replicas + (r ^ turn)))
    return lax.ppermute(block, AXES, route)


def bits_of(count):
    return [1 << b for b in range(count.bit_length() - 1)]


def cut(width, parts):
    tiles = width // LANES
    edges = [(tiles * i + parts - 1) // parts * LANES for i in range(parts + 1)]
    return list(zip(edges[:-1], edges[1:]))


def turned(dims, by):
    order = dims[::-1]
    order = order[-1:] + order[:-1]
    by = by % len(order)
    return order[by:] + order[:by]


def masks_of(order, dims):
    found = [0]
    for dim in order:
        found = found + [m ^ 1 << dims.index(dim) for m in found]
    return found


def gather_cube(blocks, orders):
    stacks = [b[None] for b in blocks]
    last = len(orders[0][0]) - 1
    for level in range(last + 1):
        others = []
        for stack, order in zip(stacks, orders):
            others.append(hop(stack, order[0][level], order[1][level]))
        if level < last:
            stacks = lax.optimization_barrier([jnp.concatenate(pair, axis=0) for pair in zip(stacks, others)])
    return list(zip(stacks, lax.optimization_barrier(others)))


def dot(a, b, over):
    return lax.dot_general(a, b, (over, ((), ())), preferred_element_type=jnp.float32)


def one_hot(mask):
    return jnp.where(mask, 1.0, 0.0).astype(jnp.bfloat16)


def pick_kernel(window, folds, group_ref, routes_ref, gates_ref, tokens_ref, cotangent_ref, *outs):
    count = tokens_ref.shape[0]
    fold = tokens_ref.shape[1] // folds
    span = 2 * CAP * folds
    routes, gates = routes_ref[...], gates_ref[...]
    ahead = one_hot(
        lax.broadcasted_iota(jnp.int32, (count, count), 0) < lax.broadcasted_iota(jnp.int32, (count, count), 1)
    )
    place = lax.broadcasted_iota(jnp.int32, (span, count), 0)
    row = place % (2 * CAP)
    slot = row % CAP
    inputs_at, scaled_at, weights = [], [], []
    for k in range(window):
        match = routes == (group_ref[0] ^ k)
        chosen = jnp.sum(jnp.where(match, 1.0, 0.0), axis=0, keepdims=True)
        scale = jnp.sum(jnp.where(match, gates, 0.0), axis=0, keepdims=True)
        rank = dot(jnp.broadcast_to(chosen, (SUBLANES, count)).astype(jnp.bfloat16), ahead, ((1,), (0,)))[:1]
        hit = (rank == slot.astype(jnp.float32)) & (chosen > 0.0)
        inputs_at.append(hit & (row < CAP))
        scaled_at.append(hit & (row >= CAP))
        weights.append(jnp.sum(jnp.where(scaled_at[-1], scale, 0.0), axis=1, keepdims=True))
    weight = jnp.concatenate(weights, axis=0)
    total = jnp.zeros((window * span, fold), jnp.float32)
    for f in range(folds):
        here = place // (2 * CAP) == f
        where = pl.ds(f * fold, fold)
        left = jnp.concatenate([one_hot(hit & here) for hit in inputs_at], axis=0)
        right = jnp.concatenate([one_hot(hit & here) for hit in scaled_at], axis=0)
        total += dot(left, tokens_ref[:, where], ((1,), (0,)))
        total += weight * dot(right, cotangent_ref[:, where], ((1,), (0,)))
    for k, out in enumerate(outs):
        out[...] = total[k * span : (k + 1) * span].astype(jnp.bfloat16)


def join_kernel(folds, edges, entries, core_ref, *refs):
    outs = refs[-len(edges) :]
    sources = refs[: -len(edges)]
    core = core_ref[0]
    rows = outs[0].shape[0]
    span = sources[0].shape[0]
    place = lax.broadcasted_iota(jnp.int32, (rows, span), 0)
    item = lax.broadcasted_iota(jnp.int32, (rows, span), 1)
    slot = item % CAP
    quarters = []
    for f in range(folds // 2):
        total = jnp.zeros((rows, sources[0].shape[1]), jnp.float32)
        for source, (flip, low, high, start) in zip(sources, entries):
            base = start + (core ^ flip) * (high - low) - low
            goal = item % (2 * CAP) // CAP * (rows // 2) + base + slot
            taken = (item // (2 * CAP) == core * (folds // 2) + f) & (place == goal) & (slot >= low) & (slot < high)
            total += dot(one_hot(taken), source[...], ((1,), (0,)))
        quarters.append(total.astype(jnp.bfloat16))
    whole = jnp.concatenate(quarters, axis=1)
    for out, (low, high) in zip(outs, edges):
        out[...] = whole[:, low:high]


class Plan:
    def __init__(self, count, places, edges, half):
        self.count = count
        self.rows = -(-count // (2 * SUBLANES)) * 2 * SUBLANES
        self.start = 2 * count - self.rows
        self.shift = count - self.start
        self.places = places
        self.chips = len(places[0][0])
        self.edges = edges
        self.half = half

    def chip(self, side, part, place):
        even, odd = self.places[part][0][place], self.places[part][1][place]
        return even if even == odd else jnp.where(side == 0, even, odd)

    def take(self, pair, low, width, scaled):
        first = self.start if scaled else 0
        found = [ref[:, first : first + self.rows, low : low + width].reshape(-1, width) for ref in pair]
        return jnp.concatenate(found, axis=0)


def in_pairs(flat, parts):
    return [[flat[(lineage * parts + p) * 2 : (lineage * parts + p) * 2 + 2] for p in range(parts)] for lineage in range(2)]


def forward(plan, pairs, core, weights, held, sems, pre):
    gate_held, up_held, down_held = held
    rows, chips, units = plan.rows, plan.chips, gate_held.shape[1]
    steps = []
    for lineage in range(2):
        for p, (low, high) in enumerate(plan.edges):
            side = core ^ lineage
            where = pl.ds(pl.multiple_of(side * plan.half + low, LANES), high - low)
            spots = [(where, slice(None)), (where, slice(None)), (slice(None), where)]
            copies = [
                pltpu.make_async_copy(w.at[at], h.at[at], sems.at[len(steps), i])
                for i, (w, h, at) in enumerate(zip(weights, held, spots))
            ]
            for copy in copies:
                copy.start()
            steps.append((lineage, p, low, high, side, where, copies))
    for lineage, p, low, high, side, where, copies in steps:
        for copy in copies:
            copy.wait()
        inputs = plan.take(pairs[lineage][p], 0, high - low, False)
        scaled = plan.take(pairs[lineage][p], 0, high - low, True)
        sums = (
            dot(inputs, gate_held[where, :], ((1,), (0,))),
            dot(inputs, up_held[where, :], ((1,), (0,))),
            dot(scaled, down_held[:, where], ((1,), (1,))),
        )
        for place in range(chips):
            m = plan.chip(side, p, place)
            for i, value in enumerate(sums):
                part = value[place * rows : (place + 1) * rows]
                pre[i, m] = part if lineage + p == 0 else pre[i, m] + part
    gate_pre, up_pre, back = [pre[i].reshape(chips * rows, units) for i in range(3)]
    total = chips * rows
    if plan.shift:
        back = pltpu.roll(back, total - plan.shift, 0)
    live = lax.broadcasted_iota(jnp.int32, (total, units), 0) % rows < plan.count
    sigmoid = 1.0 / (1.0 + jnp.exp(-gate_pre))
    active = gate_pre * sigmoid
    hidden = jnp.where(live, active * up_pre, 0.0)
    if plan.shift:
        hidden = pltpu.roll(hidden, plan.shift, 0)
    gate_delta = jnp.where(live, back * up_pre * sigmoid * (1.0 + gate_pre * (1.0 - sigmoid)), 0.0)
    up_delta = jnp.where(live, back * active, 0.0)
    return [v.astype(jnp.bfloat16).reshape(chips, rows, units) for v in (gate_delta, up_delta, hidden)]


def first_kernel(plan, core_ref, gate_ref, up_ref, down_ref, *rest):
    parts = len(plan.edges)
    pairs = in_pairs(rest[: 4 * parts], parts)
    delta_ref, hidden_ref, pre, gate_held, up_held, down_held, sems = rest[4 * parts :]
    units = gate_held.shape[1]
    held = (gate_held, up_held, down_held)
    gate_delta, up_delta, hidden = forward(plan, pairs, core_ref[0], (gate_ref, up_ref, down_ref), held, sems, pre)
    delta_ref[:, :, :units] = gate_delta
    delta_ref[:, :, units:] = up_delta
    hidden_ref[...] = hidden


def second_kernel(plans, core_ref, first_delta, first_hidden, gate_ref, up_ref, down_ref, *rest):
    first, second = plans
    parts = len(first.edges)
    first_pairs = in_pairs(rest[: 4 * parts], parts)
    second_pairs = in_pairs(rest[4 * parts : 8 * parts], parts)
    gate_out, up_out, down_out, delta_ref, hidden_ref, pre, gate_held, up_held, down_held, sems, tall, wide, tall_sem, wide_sem = rest[8 * parts :]
    core = core_ref[0]
    chips, units = second.chips, gate_held.shape[1]
    held = (gate_held, up_held, down_held)
    gate_delta, up_delta, hidden = forward(second, second_pairs, core, (gate_ref, up_ref, down_ref), held, sems, pre)
    delta_ref[:, :, :units] = gate_delta
    delta_ref[:, :, units:] = up_delta
    hidden_ref[...] = hidden
    flying = [[], []]
    turn = 0
    for lineage in range(2):
        side = core ^ lineage
        for p, (begin, end) in enumerate(first.edges):
            order = [first.chip(side, p, place) for place in range(chips)]
            delta = jnp.concatenate([first_delta[m] for m in order] + [delta_ref[m] for m in order], axis=0)
            hidden = jnp.concatenate([first_hidden[m] for m in order] + [hidden_ref[m] for m in order], axis=0)
            for low, high in cut(end - begin, -(-(end - begin) // PIECE)):
                width = high - low
                where = pl.ds(pl.multiple_of(side * first.half + begin + low, LANES), width)
                slot = turn % 2
                turn += 1
                for copy in flying[slot]:
                    copy.wait()

                def rows_of(scaled):
                    return jnp.concatenate(
                        (
                            first.take(first_pairs[lineage][p], low, width, scaled),
                            second.take(second_pairs[lineage][p], low, width, scaled),
                        ),
                        axis=0,
                    )

                both = dot(rows_of(False), delta, ((0,), (0,))).astype(jnp.bfloat16)
                tall[slot, 0, :width, :] = both[:, :units]
                tall[slot, 1, :width, :] = both[:, units:]
                wide[slot, :, :width] = dot(hidden, rows_of(True), ((0,), (0,))).astype(jnp.bfloat16)
                copies = [
                    pltpu.make_async_copy(tall.at[slot, 0, pl.ds(0, width), :], gate_out.at[where, :], tall_sem.at[slot, 0]),
                    pltpu.make_async_copy(tall.at[slot, 1, pl.ds(0, width), :], up_out.at[where, :], tall_sem.at[slot, 1]),
                    pltpu.make_async_copy(wide.at[slot, :, pl.ds(0, width)], down_out.at[:, where], wide_sem.at[slot]),
                ]
                for copy in copies:
                    copy.start()
                flying[slot] = copies
    for copies in flying:
        for copy in copies:
            copy.wait()


def on_device(tokens, cotangent, routes, route_gates, gate_weight, up_weight, down_weight):
    units = gate_weight.shape[2]
    slices = HIDDEN_SIZE // units
    window = lax.axis_size("expert") // slices
    width = tokens.shape[1]
    half = width // 2
    me = lax.axis_index("expert").astype(jnp.int32)
    group = (me // slices).reshape(1)
    core = (me % 2).reshape(1)
    smem = pl.BlockSpec(memory_space=pltpu.SMEM)
    vmem = pl.BlockSpec(memory_space=pltpu.VMEM)
    hbm = pl.BlockSpec(memory_space=pl.ANY)

    def near(arrays):
        return [pltpu.with_memory_space_constraint(x, pltpu.VMEM) for x in arrays]

    params = pltpu.CompilerParams(vmem_limit_bytes=KERNEL_VMEM)
    folds = 2
    while 2 * CAP * folds % SUBLANES:
        folds *= 2
    span = 2 * CAP * folds
    picked = pl.pallas_call(
        functools.partial(pick_kernel, window, folds),
        out_shape=(jax.ShapeDtypeStruct((span, width // folds), jnp.bfloat16),) * window,
        in_specs=[smem] + [vmem] * 4,
        out_specs=(vmem,) * window,
        compiler_params=params,
    )(group, routes.T, route_gates.T, tokens, cotangent)
    weights = [pltpu.with_memory_space_constraint(w[0], pltpu.HBM) for w in (gate_weight, up_weight, down_weight)]
    partner = (1, 0)
    landed = [picked[0]]
    for k in range(1, window):
        landed.append(hop(picked[k], (k * slices, 0)))
    pairs = []
    for block in landed:
        pairs.append((block, hop(block, partner)))

    dims = [(0, m) for m in bits_of(lax.axis_size("dp"))] + [(m, 0) for m in bits_of(slices)[1:]]
    tiles = half // LANES
    major = -(-2 * tiles // len(dims)) * LANES
    edges = [(0, major), (major, half)]
    orders = [(turned(dims, 0), turned(dims, 2)), (turned(dims, 1), turned(dims, 1))]
    places = [tuple(masks_of(o, dims) for o in order) for order in orders]
    main = CAP // SUBLANES * SUBLANES
    early = [(0, 0, main, 0)]
    late = [(k, 0, CAP, (k - 1) * 2 * CAP) for k in range(1, window)]
    if main < CAP:
        late.append((0, main, CAP, (window - 1) * 2 * CAP))
    plans, operands, gathered = [], [], []
    for taken in (early, late):
        count = sum(2 * (high - low) for _, low, high, _ in taken)
        count += -count % (SUBLANES // 2)
        sources = [x for k, _, _, _ in taken for x in pairs[k]]
        entries = [(flip, low, high, start) for _, low, high, start in taken for flip in range(2)]
        blocks = pl.pallas_call(
            functools.partial(join_kernel, folds, edges, entries),
            out_shape=tuple(jax.ShapeDtypeStruct((2 * count, high - low), jnp.bfloat16) for low, high in edges),
            in_specs=[smem] + [vmem] * len(sources),
            out_specs=(vmem,) * len(edges),
            compiler_params=params,
        )(core, *near(sources))
        halves = gather_cube(blocks, orders)
        gathered.append(halves)
        stacks = [s for pair in halves for s in pair]
        crossed = []
        for stack in stacks:
            crossed.append(hop(stack, partner))
        operands.append(stacks + crossed)
        plans.append(Plan(count, places, edges, half))

    chips = plans[0].chips

    def delta_shapes(plan, make):
        return [make((chips, plan.rows, 2 * units), jnp.bfloat16), make((chips, plan.rows, units), jnp.bfloat16)]

    def forward_scratch(plan):
        return [
            pltpu.VMEM((3, chips, plan.rows, units), jnp.float32),
            pltpu.VMEM((width, units), jnp.bfloat16),
            pltpu.VMEM((width, units), jnp.bfloat16),
            pltpu.VMEM((units, width), jnp.bfloat16),
            pltpu.SemaphoreType.DMA((2 * len(edges), 3)),
        ]

    flops = [6 * chips * plan.rows * width * units for plan in plans]
    operands[0], _ = lax.optimization_barrier((operands[0], gathered[1][0][0]))
    first = pl.pallas_call(
        functools.partial(first_kernel, plans[0]),
        out_shape=tuple(delta_shapes(plans[0], jax.ShapeDtypeStruct)),
        in_specs=[smem] + [hbm] * 3 + [vmem] * len(operands[0]),
        out_specs=(vmem, vmem),
        scratch_shapes=forward_scratch(plans[0]),
        cost_estimate=pl.CostEstimate(flops=flops[0], bytes_accessed=6 * width * units, transcendentals=0),
        compiler_params=params,
    )(core, *weights, *near(operands[0]))
    grads = pl.pallas_call(
        functools.partial(second_kernel, plans),
        out_shape=(
            jax.ShapeDtypeStruct((width, units), jnp.bfloat16),
            jax.ShapeDtypeStruct((width, units), jnp.bfloat16),
            jax.ShapeDtypeStruct((units, width), jnp.bfloat16),
        ),
        in_specs=[smem] + [vmem] * 2 + [hbm] * 3 + [vmem] * (len(operands[0]) + len(operands[1])),
        out_specs=(hbm, hbm, hbm),
        scratch_shapes=delta_shapes(plans[1], pltpu.VMEM)
        + forward_scratch(plans[1])
        + [
            pltpu.VMEM((2, 2, PIECE, units), jnp.bfloat16),
            pltpu.VMEM((2, units, PIECE), jnp.bfloat16),
            pltpu.SemaphoreType.DMA((2, 2)),
            pltpu.SemaphoreType.DMA((2,)),
        ],
        cost_estimate=pl.CostEstimate(flops=2 * sum(flops), bytes_accessed=12 * width * units, transcendentals=0),
        compiler_params=params,
    )(core, *near(first), *weights, *near(operands[0]), *near(operands[1]))
    return tuple(g[None] for g in grads)


def solution(mesh):
    split = P(("expert", "dp"), None)
    held = P("expert", None, None)

    return jax.shard_map(
        on_device,
        mesh=mesh,
        in_specs=(split, split, split, split, held, held, held),
        out_specs=(held, held, held),
        check_vma=False,
    )
```

profile of v0, /device:TPU:0, one launch (start us, length us, event | category | flops | bytes accessed | tf_op | source)
XLA Modules:
  0.0 89.4 jit_solution(6413536996113064033)
XLA Ops:
  0.7 1.5 %copy-done = bf16[128,7168]{1,0:T(8,128)(2,1)S(1)} copy-done((bf16[128,7168]{1,0:T(8,128)(2,1)S(1)}, bf16[128,7168]{1,0:T(8,128)(2,1)}, u32[]{:S(2)}) %copy-start) | copy-done | bytes 1835032
  2.1 1.5 %copy-done.1 = bf16[128,7168]{1,0:T(8,128)(2,1)S(1)} copy-done((bf16[128,7168]{1,0:T(8,128)(2,1)S(1)}, bf16[128,7168]{1,0:T(8,128)(2,1)}, u32[]{:S(2)}) %copy-start.1) | copy-done | bytes 1835032
  3.6 0.7 copy-done.2
  4.3 0.7 copy-done.3
  5.0 1.4 %shard_map.94 = (bf16[72,1792]{1,0:T(8,128)(2,1)S(1)}, bf16[72,1792]{1,0:T(8,128)(2,1)S(1)}) custom-call(s32[1]{0:T(128)} %bitcast.4.group_ref, s32[8,128]{1,0:T(8,128)S(1)} %bitcast.22, f32[8,128]{1,0:T(8,128)S(1)} %bitcast.23, bf16[128,7168]{1,0:T(8,128)(2,1)S(1)} %copy-done, bf16[128,7168]{1,0:T(8,128)(2,1)S(1)} %copy-done.1), custom_call_target="tpu_custom_call" | custom-call | tf_op jit(solution)/shard_map/pallas_call | solution.py:291
  6.4 0.6 collective-permute-start
  7.0 3.7 %collective-permute-start.11 = (bf16[72,1792]{1,0:T(8,128)(2,1)S(1)}, bf16[72,1792]{1,0:T(8,128)(2,1)S(1)}, u32[]{:S(2)}, u32[]{:S(2)}) collective-permute-start(bf16[72,1792]{1,0:T(8,128)(2,1)S(1)} %get-tuple-element.43), channel_id=1, source_target_pairs={{0,16},{1,17},{2,18},{3,19},{4,20},{5,21},{6,22},{7,23},{8,24},{9,... | collective-permute-start | bytes 774152 | tf_op jit(solution)/shard_map/ppermute | solution.py:28
  10.7 0.0 collective-permute-done.refs_1_.refs_3_
  10.7 0.3 shard_map.95
  11.0 1.6 %collective-permute-start.2 = (bf16[1,32,1152]{2,1,0:T(8,128)(2,1)S(1)}, bf16[1,32,1152]{2,1,0:T(8,128)(2,1)S(1)}, u32[]{:S(2)}, u32[]{:S(2)}) collective-permute-start(bf16[1,32,1152]{2,1,0:T(8,128)(2,1)S(1)} %bitcast.20), channel_id=1, source_target_pairs={{0,8},{1,9},{2,10},{3,11},{4,12},{5,13},{6,14},{7,15},{8,0},{9,1},... | collective-permute-start | bytes 221192 | tf_op jit(solution)/shard_map/ppermute | solution.py:28
  12.6 10.4 %collective-permute-done.11.refs_0_ = bf16[72,1792]{1,0:T(8,128)(2,1)S(1)} collective-permute-done((bf16[72,1792]{1,0:T(8,128)(2,1)S(1)}, bf16[72,1792]{1,0:T(8,128)(2,1)S(1)}, u32[]{:S(2)}, u32[]{:S(2)}) %collective-permute-start.11) | collective-permute-done | bytes 258080 | tf_op jit(solution)/shard_map/ppermute | solution.py:28
  23.0 0.0 collective-permute-start.12
  23.0 1.5 %collective-permute-start.1 = (bf16[1,32,2432]{2,1,0:T(8,128)(2,1)S(1)}, bf16[1,32,2432]{2,1,0:T(8,128)(2,1)S(1)}, u32[]{:S(2)}, u32[]{:S(2)}) collective-permute-start(bf16[1,32,2432]{2,1,0:T(8,128)(2,1)S(1)} %bitcast.16), channel_id=1, source_target_pairs={{0,1},{1,0},{2,6},{3,7},{4,5},{5,4},{6,2},{7,3},{8,9},{9,8},{10,14... | collective-permute-start | bytes 466952 | tf_op jit(solution)/shard_map/ppermute | solution.py:28
  24.5 0.0 collective-permute-done.2
  24.6 0.0 collective-permute-done.12.refs_1_
  24.6 0.5 shard_map.96
  25.1 0.8 collective-permute-start.14
  25.9 2.3 %collective-permute-done.1 = bf16[1,32,2432]{2,1,0:T(8,128)(2,1)S(1)} collective-permute-done((bf16[1,32,2432]{2,1,0:T(8,128)(2,1)S(1)}, bf16[1,32,2432]{2,1,0:T(8,128)(2,1)S(1)}, u32[]{:S(2)}, u32[]{:S(2)}) %collective-permute-start.1) | collective-permute-done | bytes 155680 | tf_op jit(solution)/shard_map/ppermute | solution.py:28
  28.3 1.6 %collective-permute-start.4 = (bf16[2,32,1152]{2,1,0:T(8,128)(2,1)S(1)}, bf16[2,32,1152]{2,1,0:T(8,128)(2,1)S(1)}, u32[]{:S(2)}, u32[]{:S(2)}) collective-permute-start(bf16[2,32,1152]{2,1,0:T(8,128)(2,1)S(1)} %pad_maximum_fusion.7), channel_id=1, source_target_pairs={{0,4},{1,5},{2,6},{3,7},{4,0},{5,1},{6,2},{7,3},{8,12},{9,13},{10,... | collective-permute-start | bytes 442376 | tf_op jit(solution)/shard_map/ppermute | solution.py:28
  29.9 0.7 collective-permute-start.3
  30.6 1.5 %collective-permute-start.13 = (bf16[1,40,2432]{2,1,0:T(8,128)(2,1)S(1)}, bf16[1,40,2432]{2,1,0:T(8,128)(2,1)S(1)}, u32[]{:S(2)}, u32[]{:S(2)}) collective-permute-start(bf16[1,40,2432]{2,1,0:T(8,128)(2,1)S(1)} %bitcast.14), channel_id=1, source_target_pairs={{0,1},{1,0},{2,6},{3,7},{4,5},{5,4},{6,2},{7,3},{8,9},{9,8},{10,14... | collective-permute-start | bytes 583688 | tf_op jit(solution)/shard_map/ppermute | solution.py:28
  32.2 5.1 %collective-permute-done.13 = bf16[1,40,2432]{2,1,0:T(8,128)(2,1)S(1)} collective-permute-done((bf16[1,40,2432]{2,1,0:T(8,128)(2,1)S(1)}, bf16[1,40,2432]{2,1,0:T(8,128)(2,1)S(1)}, u32[]{:S(2)}, u32[]{:S(2)}) %collective-permute-start.13) | collective-permute-done | bytes 194592 | tf_op jit(solution)/shard_map/ppermute | solution.py:28
  37.3 0.5 collective-permute-start.16
  37.9 0.7 collective-permute-start.15
  38.6 4.3 %collective-permute-done.16 = bf16[2,40,1152]{2,1,0:T(8,128)(2,1)S(1)} collective-permute-done((bf16[2,40,1152]{2,1,0:T(8,128)(2,1)S(1)}, bf16[2,40,1152]{2,1,0:T(8,128)(2,1)S(1)}, u32[]{:S(2)}, u32[]{:S(2)}) %collective-permute-start.16) | collective-permute-done | bytes 184352 | tf_op jit(solution)/shard_map/ppermute | solution.py:28
  43.0 2.6 %collective-permute-done.15 = bf16[2,40,2432]{2,1,0:T(8,128)(2,1)S(1)} collective-permute-done((bf16[2,40,2432]{2,1,0:T(8,128)(2,1)S(1)}, bf16[2,40,2432]{2,1,0:T(8,128)(2,1)S(1)}, u32[]{:S(2)}, u32[]{:S(2)}) %collective-permute-start.15) | collective-permute-done | bytes 389152 | tf_op jit(solution)/shard_map/ppermute | solution.py:28
  45.6 0.1 pad_maximum_fusion.rest_8_
  45.7 1.6 %collective-permute-start.17 = (bf16[4,40,2432]{2,1,0:T(8,128)(2,1)S(1)}, bf16[4,40,2432]{2,1,0:T(8,128)(2,1)S(1)}, u32[]{:S(2)}, u32[]{:S(2)}) collective-permute-start(bf16[4,40,2432]{2,1,0:T(8,128)(2,1)S(1)} %pad_maximum_fusion.rest_8_), channel_id=1, source_target_pairs={{0,4},{1,5},{2,10},{3,11},{4,0},{5,1},{6,14},{7,15},{8,12},{9,13},... | collective-permute-start | bytes 2334728 | tf_op jit(solution)/shard_map/ppermute | solution.py:28
  47.3 0.1 pad_maximum_fusion.1.rest_0_
  47.4 0.5 collective-permute-start.5
  47.9 1.5 %collective-permute-start.18 = (bf16[4,40,1152]{2,1,0:T(8,128)(2,1)S(1)}, bf16[4,40,1152]{2,1,0:T(8,128)(2,1)S(1)}, u32[]{:S(2)}, u32[]{:S(2)}) collective-permute-start(bf16[4,40,1152]{2,1,0:T(8,128)(2,1)S(1)} %pad_maximum_fusion.3.rest_10_), channel_id=1, source_target_pairs={{0,1},{1,0},{2,3},{3,2},{4,5},{5,4},{6,7},{7,6},{8,9},{9,8},{10,11... | collective-permute-start | bytes 1105928 | tf_op jit(solution)/shard_map/ppermute | solution.py:28
  49.5 0.5 collective-permute-start.6
  49.9 9.4 %collective-permute-done.18.rest_11_ = bf16[4,40,1152]{2,1,0:T(8,128)(2,1)S(1)} collective-permute-done((bf16[4,40,1152]{2,1,0:T(8,128)(2,1)S(1)}, bf16[4,40,1152]{2,1,0:T(8,128)(2,1)S(1)}, u32[]{:S(2)}, u32[]{:S(2)}) %collective-permute-start.18) | collective-permute-done | bytes 368672 | tf_op jit(solution)/shard_map/ppermute | solution.py:28
  59.4 0.0 collective-permute-start.9
  59.4 0.0 collective-permute-done.17.rest_9_
  59.4 0.5 collective-permute-start.19
  59.9 2.9 %collective-permute-done.6.rest_3_ = bf16[4,32,1152]{2,1,0:T(8,128)(2,1)S(1)} collective-permute-done((bf16[4,32,1152]{2,1,0:T(8,128)(2,1)S(1)}, bf16[4,32,1152]{2,1,0:T(8,128)(2,1)S(1)}, u32[]{:S(2)}, u32[]{:S(2)}) %collective-permute-start.6) | collective-permute-done | bytes 294944 | tf_op jit(solution)/shard_map/ppermute | solution.py:28
  62.8 0.0 collective-permute-start.20
  62.8 1.5 %collective-permute-done.5.rest_1_ = bf16[4,32,2432]{2,1,0:T(8,128)(2,1)S(1)} collective-permute-done((bf16[4,32,2432]{2,1,0:T(8,128)(2,1)S(1)}, bf16[4,32,2432]{2,1,0:T(8,128)(2,1)S(1)}, u32[]{:S(2)}, u32[]{:S(2)}) %collective-permute-start.5) | collective-permute-done | bytes 622624 | tf_op jit(solution)/shard_map/ppermute | solution.py:28
  64.3 0.0 collective-permute-start.8
  64.3 0.0 collective-permute-done.9.rest_6_
  64.3 0.5 collective-permute-start.10
  64.8 0.0 collective-permute-done.7.rest_4_
  64.8 0.1 collective-permute-start.21
  64.9 1.9 %collective-permute-done.10.rest_7_ = bf16[4,32,1152]{2,1,0:T(8,128)(2,1)S(1)} collective-permute-done((bf16[4,32,1152]{2,1,0:T(8,128)(2,1)S(1)}, bf16[4,32,1152]{2,1,0:T(8,128)(2,1)S(1)}, u32[]{:S(2)}, u32[]{:S(2)}) %collective-permute-start.10) | collective-permute-done | bytes 294944 | tf_op jit(solution)/shard_map/ppermute | solution.py:28
  66.8 0.1 collective-permute-start.22
  66.9 5.7 %shard_map.97 = (bf16[8,16,512]{2,1,0:T(8,128)(2,1)S(1)}, bf16[8,16,256]{2,1,0:T(8,128)(2,1)S(1)}) custom-call(s32[1]{0:T(128)} %bitcast.core_ref, bf16[7168,256]{1,0:T(8,128)(2,1)} %bitcast.24, bf16[7168,256]{1,0:T(8,128)(2,1)} %bitcast.26, bf16[256,7168]{1,0:T(8,128)(2,1)} %bitcast.28, bf16[4,32,2432]{2,1,0:T(8,128)(2,1)S(1)} %pad_maximum_fusion.1.rest_0_, ...), custom_call_target="tpu_custom_call" | custom-call | flops 1409286144 | bytes 11010048 | tf_op jit(solution)/shard_map/pallas_call | solution.py:356
  72.7 16.5 %shard_map.98 = (bf16[7168,256]{1,0:T(8,128)(2,1)}, bf16[7168,256]{1,0:T(8,128)(2,1)}, bf16[256,7168]{1,0:T(8,128)(2,1)}) custom-call(s32[1]{0:T(128)} %bitcast.core_ref, bf16[8,16,512]{2,1,0:T(8,128)(2,1)S(1)} %get-tuple-element.57.first_delta, bf16[8,16,256]{2,1,0:T(8,128)(2,1)S(1)} %get-tuple-element.58.first_hidden, bf16[7168,256]{1,0:T(8,128)(2,1)} %bitcast.25, ...), custom_call_target="tpu_custom_call" | custom-call | flops 8455716864 | bytes 22020096 | tf_op jit(solution)/shard_map/pallas_call | solution.py:365
  (19 shorter events, 0.2 us)
Async XLA Ops:
  0.6 1.5 %copy-start = (bf16[128,7168]{1,0:T(8,128)(2,1)S(1)}, bf16[128,7168]{1,0:T(8,128)(2,1)}, u32[]{:S(2)}) copy-start(bf16[128,7168]{1,0:T(8,128)(2,1)} %tokens_ref.1) | copy-start | bytes 5505028
  2.1 1.5 %copy-start.1 = (bf16[128,7168]{1,0:T(8,128)(2,1)S(1)}, bf16[128,7168]{1,0:T(8,128)(2,1)}, u32[]{:S(2)}) copy-start(bf16[128,7168]{1,0:T(8,128)(2,1)} %cotangent_ref.1) | copy-start | bytes 5505028
  3.6 0.7 copy-start.2
  4.3 0.7 copy-start.3
  6.4 4.2 %collective-permute-start = (bf16[72,1792]{1,0:T(8,128)(2,1)S(1)}, bf16[72,1792]{1,0:T(8,128)(2,1)S(1)}, u32[]{:S(2)}, u32[]{:S(2)}) collective-permute-start(bf16[72,1792]{1,0:T(8,128)(2,1)S(1)} %get-tuple-element.34.refs_0_.refs_2_), channel_id=1, source_target_pairs={{0,2},{1,3},{2,0},{3,1},{4,6},{5,7},{6,4},{7,5},{8,10},{9,11},{10,... | collective-permute-start | bytes 774152 | tf_op jit(solution)/shard_map/ppermute | solution.py:28
  7.0 16.0 %collective-permute-start.11 = (bf16[72,1792]{1,0:T(8,128)(2,1)S(1)}, bf16[72,1792]{1,0:T(8,128)(2,1)S(1)}, u32[]{:S(2)}, u32[]{:S(2)}) collective-permute-start(bf16[72,1792]{1,0:T(8,128)(2,1)S(1)} %get-tuple-element.43), channel_id=1, source_target_pairs={{0,16},{1,17},{2,18},{3,19},{4,20},{5,21},{6,22},{7,23},{8,24},{9,... | collective-permute-start | bytes 774152 | tf_op jit(solution)/shard_map/ppermute | solution.py:28
  11.0 13.6 %collective-permute-start.2 = (bf16[1,32,1152]{2,1,0:T(8,128)(2,1)S(1)}, bf16[1,32,1152]{2,1,0:T(8,128)(2,1)S(1)}, u32[]{:S(2)}, u32[]{:S(2)}) collective-permute-start(bf16[1,32,1152]{2,1,0:T(8,128)(2,1)S(1)} %bitcast.20), channel_id=1, source_target_pairs={{0,8},{1,9},{2,10},{3,11},{4,12},{5,13},{6,14},{7,15},{8,0},{9,1},... | collective-permute-start | bytes 221192 | tf_op jit(solution)/shard_map/ppermute | solution.py:28
  23.0 1.6 %collective-permute-start.12 = (bf16[72,1792]{1,0:T(8,128)(2,1)S(1)}, bf16[72,1792]{1,0:T(8,128)(2,1)S(1)}, u32[]{:S(2)}, u32[]{:S(2)}) collective-permute-start(bf16[72,1792]{1,0:T(8,128)(2,1)S(1)} %collective-permute-done.11.refs_0_), channel_id=1, source_target_pairs={{0,2},{1,3},{2,0},{3,1},{4,6},{5,7},{6,4},{7,5},{8,10},{9,11},{10,... | collective-permute-start | bytes 774152 | tf_op jit(solution)/shard_map/ppermute | solution.py:28
  23.0 5.2 %collective-permute-start.1 = (bf16[1,32,2432]{2,1,0:T(8,128)(2,1)S(1)}, bf16[1,32,2432]{2,1,0:T(8,128)(2,1)S(1)}, u32[]{:S(2)}, u32[]{:S(2)}) collective-permute-start(bf16[1,32,2432]{2,1,0:T(8,128)(2,1)S(1)} %bitcast.16), channel_id=1, source_target_pairs={{0,1},{1,0},{2,6},{3,7},{4,5},{5,4},{6,2},{7,3},{8,9},{9,8},{10,14... | collective-permute-start | bytes 466952 | tf_op jit(solution)/shard_map/ppermute | solution.py:28
  25.1 7.0 %collective-permute-start.14 = (bf16[1,40,1152]{2,1,0:T(8,128)(2,1)S(1)}, bf16[1,40,1152]{2,1,0:T(8,128)(2,1)S(1)}, u32[]{:S(2)}, u32[]{:S(2)}) collective-permute-start(bf16[1,40,1152]{2,1,0:T(8,128)(2,1)S(1)} %bitcast.18), channel_id=1, source_target_pairs={{0,8},{1,9},{2,10},{3,11},{4,12},{5,13},{6,14},{7,15},{8,0},{9,1},... | collective-permute-start | bytes 276488 | tf_op jit(solution)/shard_map/ppermute | solution.py:28
  28.3 10.3 %collective-permute-start.4 = (bf16[2,32,1152]{2,1,0:T(8,128)(2,1)S(1)}, bf16[2,32,1152]{2,1,0:T(8,128)(2,1)S(1)}, u32[]{:S(2)}, u32[]{:S(2)}) collective-permute-start(bf16[2,32,1152]{2,1,0:T(8,128)(2,1)S(1)} %pad_maximum_fusion.7), channel_id=1, source_target_pairs={{0,4},{1,5},{2,6},{3,7},{4,0},{5,1},{6,2},{7,3},{8,12},{9,13},{10,... | collective-permute-start | bytes 442376 | tf_op jit(solution)/shard_map/ppermute | solution.py:28
  29.9 17.4 %collective-permute-start.3 = (bf16[2,32,2432]{2,1,0:T(8,128)(2,1)S(1)}, bf16[2,32,2432]{2,1,0:T(8,128)(2,1)S(1)}, u32[]{:S(2)}, u32[]{:S(2)}) collective-permute-start(bf16[2,32,2432]{2,1,0:T(8,128)(2,1)S(1)} %pad_maximum_fusion.4), channel_id=1, source_target_pairs={{0,8},{1,9},{2,3},{3,2},{4,12},{5,13},{6,7},{7,6},{8,0},{9,1},{10,... | collective-permute-start | bytes 933896 | tf_op jit(solution)/shard_map/ppermute | solution.py:28
  30.6 6.6 %collective-permute-start.13 = (bf16[1,40,2432]{2,1,0:T(8,128)(2,1)S(1)}, bf16[1,40,2432]{2,1,0:T(8,128)(2,1)S(1)}, u32[]{:S(2)}, u32[]{:S(2)}) collective-permute-start(bf16[1,40,2432]{2,1,0:T(8,128)(2,1)S(1)} %bitcast.14), channel_id=1, source_target_pairs={{0,1},{1,0},{2,6},{3,7},{4,5},{5,4},{6,2},{7,3},{8,9},{9,8},{10,14... | collective-permute-start | bytes 583688 | tf_op jit(solution)/shard_map/ppermute | solution.py:28
  37.3 5.6 %collective-permute-start.16 = (bf16[2,40,1152]{2,1,0:T(8,128)(2,1)S(1)}, bf16[2,40,1152]{2,1,0:T(8,128)(2,1)S(1)}, u32[]{:S(2)}, u32[]{:S(2)}) collective-permute-start(bf16[2,40,1152]{2,1,0:T(8,128)(2,1)S(1)} %pad_maximum_fusion.6), channel_id=1, source_target_pairs={{0,4},{1,5},{2,6},{3,7},{4,0},{5,1},{6,2},{7,3},{8,12},{9,13},{10,... | collective-permute-start | bytes 552968 | tf_op jit(solution)/shard_map/ppermute | solution.py:28
  37.9 7.7 %collective-permute-start.15 = (bf16[2,40,2432]{2,1,0:T(8,128)(2,1)S(1)}, bf16[2,40,2432]{2,1,0:T(8,128)(2,1)S(1)}, u32[]{:S(2)}, u32[]{:S(2)}) collective-permute-start(bf16[2,40,2432]{2,1,0:T(8,128)(2,1)S(1)} %pad_maximum_fusion.2), channel_id=1, source_target_pairs={{0,8},{1,9},{2,3},{3,2},{4,12},{5,13},{6,7},{7,6},{8,0},{9,1},{10,... | collective-permute-start | bytes 1167368 | tf_op jit(solution)/shard_map/ppermute | solution.py:28
  45.7 13.7 %collective-permute-start.17 = (bf16[4,40,2432]{2,1,0:T(8,128)(2,1)S(1)}, bf16[4,40,2432]{2,1,0:T(8,128)(2,1)S(1)}, u32[]{:S(2)}, u32[]{:S(2)}) collective-permute-start(bf16[4,40,2432]{2,1,0:T(8,128)(2,1)S(1)} %pad_maximum_fusion.rest_8_), channel_id=1, source_target_pairs={{0,4},{1,5},{2,10},{3,11},{4,0},{5,1},{6,14},{7,15},{8,12},{9,13},... | collective-permute-start | bytes 2334728 | tf_op jit(solution)/shard_map/ppermute | solution.py:28
  47.4 16.9 %collective-permute-start.5 = (bf16[4,32,2432]{2,1,0:T(8,128)(2,1)S(1)}, bf16[4,32,2432]{2,1,0:T(8,128)(2,1)S(1)}, u32[]{:S(2)}, u32[]{:S(2)}) collective-permute-start(bf16[4,32,2432]{2,1,0:T(8,128)(2,1)S(1)} %pad_maximum_fusion.1.rest_0_), channel_id=1, source_target_pairs={{0,4},{1,5},{2,10},{3,11},{4,0},{5,1},{6,14},{7,15},{8,12},{9,13},... | collective-permute-start | bytes 1867784 | tf_op jit(solution)/shard_map/ppermute | solution.py:28
  47.9 11.5 %collective-permute-start.18 = (bf16[4,40,1152]{2,1,0:T(8,128)(2,1)S(1)}, bf16[4,40,1152]{2,1,0:T(8,128)(2,1)S(1)}, u32[]{:S(2)}, u32[]{:S(2)}) collective-permute-start(bf16[4,40,1152]{2,1,0:T(8,128)(2,1)S(1)} %pad_maximum_fusion.3.rest_10_), channel_id=1, source_target_pairs={{0,1},{1,0},{2,3},{3,2},{4,5},{5,4},{6,7},{7,6},{8,9},{9,8},{10,11... | collective-permute-start | bytes 1105928 | tf_op jit(solution)/shard_map/ppermute | solution.py:28
  49.5 13.3 %collective-permute-start.6 = (bf16[4,32,1152]{2,1,0:T(8,128)(2,1)S(1)}, bf16[4,32,1152]{2,1,0:T(8,128)(2,1)S(1)}, u32[]{:S(2)}, u32[]{:S(2)}) collective-permute-start(bf16[4,32,1152]{2,1,0:T(8,128)(2,1)S(1)} %pad_maximum_fusion.5.rest_2_), channel_id=1, source_target_pairs={{0,1},{1,0},{2,3},{3,2},{4,5},{5,4},{6,7},{7,6},{8,9},{9,8},{10,11... | collective-permute-start | bytes 884744 | tf_op jit(solution)/shard_map/ppermute | solution.py:28
  49.9 14.9 %collective-permute-start.7 = (bf16[4,32,2432]{2,1,0:T(8,128)(2,1)S(1)}, bf16[4,32,2432]{2,1,0:T(8,128)(2,1)S(1)}, u32[]{:S(2)}, u32[]{:S(2)}) collective-permute-start(bf16[4,32,2432]{2,1,0:T(8,128)(2,1)S(1)} %pad_maximum_fusion.1.rest_0_), channel_id=1, source_target_pairs={{0,2},{1,3},{2,0},{3,1},{4,6},{5,7},{6,4},{7,5},{8,10},{9,11},{10,... | collective-permute-start | bytes 1867784 | tf_op jit(solution)/shard_map/ppermute | solution.py:28
  59.4 5.0 %collective-permute-start.9 = (bf16[4,32,1152]{2,1,0:T(8,128)(2,1)S(1)}, bf16[4,32,1152]{2,1,0:T(8,128)(2,1)S(1)}, u32[]{:S(2)}, u32[]{:S(2)}) collective-permute-start(bf16[4,32,1152]{2,1,0:T(8,128)(2,1)S(1)} %pad_maximum_fusion.5.rest_2_), channel_id=1, source_target_pairs={{0,2},{1,3},{2,0},{3,1},{4,6},{5,7},{6,4},{7,5},{8,10},{9,11},{10,... | collective-permute-start | bytes 884744 | tf_op jit(solution)/shard_map/ppermute | solution.py:28
  59.4 13.3 %collective-permute-start.19 = (bf16[4,40,2432]{2,1,0:T(8,128)(2,1)S(1)}, bf16[4,40,2432]{2,1,0:T(8,128)(2,1)S(1)}, u32[]{:S(2)}, u32[]{:S(2)}) collective-permute-start(bf16[4,40,2432]{2,1,0:T(8,128)(2,1)S(1)} %pad_maximum_fusion.rest_8_), channel_id=1, source_target_pairs={{0,2},{1,3},{2,0},{3,1},{4,6},{5,7},{6,4},{7,5},{8,10},{9,11},{10,... | collective-permute-start | bytes 2334728 | tf_op jit(solution)/shard_map/ppermute | solution.py:28
  62.8 9.9 %collective-permute-start.20 = (bf16[4,40,2432]{2,1,0:T(8,128)(2,1)S(1)}, bf16[4,40,2432]{2,1,0:T(8,128)(2,1)S(1)}, u32[]{:S(2)}, u32[]{:S(2)}) collective-permute-start(bf16[4,40,2432]{2,1,0:T(8,128)(2,1)S(1)} %collective-permute-done.17.rest_9_), channel_id=1, source_target_pairs={{0,2},{1,3},{2,0},{3,1},{4,6},{5,7},{6,4},{7,5},{8,10},{9,11},{10,... | collective-permute-start | bytes 2334728 | tf_op jit(solution)/shard_map/ppermute | solution.py:28
  64.3 2.6 %collective-permute-start.8 = (bf16[4,32,2432]{2,1,0:T(8,128)(2,1)S(1)}, bf16[4,32,2432]{2,1,0:T(8,128)(2,1)S(1)}, u32[]{:S(2)}, u32[]{:S(2)}) collective-permute-start(bf16[4,32,2432]{2,1,0:T(8,128)(2,1)S(1)} %collective-permute-done.5.rest_1_), channel_id=1, source_target_pairs={{0,2},{1,3},{2,0},{3,1},{4,6},{5,7},{6,4},{7,5},{8,10},{9,11},{10,... | collective-permute-start | bytes 1867784 | tf_op jit(solution)/shard_map/ppermute | solution.py:28
  64.3 2.5 %collective-permute-start.10 = (bf16[4,32,1152]{2,1,0:T(8,128)(2,1)S(1)}, bf16[4,32,1152]{2,1,0:T(8,128)(2,1)S(1)}, u32[]{:S(2)}, u32[]{:S(2)}) collective-permute-start(bf16[4,32,1152]{2,1,0:T(8,128)(2,1)S(1)} %collective-permute-done.6.rest_3_), channel_id=1, source_target_pairs={{0,2},{1,3},{2,0},{3,1},{4,6},{5,7},{6,4},{7,5},{8,10},{9,11},{10,... | collective-permute-start | bytes 884744 | tf_op jit(solution)/shard_map/ppermute | solution.py:28
  64.8 7.8 %collective-permute-start.21 = (bf16[4,40,1152]{2,1,0:T(8,128)(2,1)S(1)}, bf16[4,40,1152]{2,1,0:T(8,128)(2,1)S(1)}, u32[]{:S(2)}, u32[]{:S(2)}) collective-permute-start(bf16[4,40,1152]{2,1,0:T(8,128)(2,1)S(1)} %pad_maximum_fusion.3.rest_10_), channel_id=1, source_target_pairs={{0,2},{1,3},{2,0},{3,1},{4,6},{5,7},{6,4},{7,5},{8,10},{9,11},{10,... | collective-permute-start | bytes 1105928 | tf_op jit(solution)/shard_map/ppermute | solution.py:28
  66.8 5.9 %collective-permute-start.22 = (bf16[4,40,1152]{2,1,0:T(8,128)(2,1)S(1)}, bf16[4,40,1152]{2,1,0:T(8,128)(2,1)S(1)}, u32[]{:S(2)}, u32[]{:S(2)}) collective-permute-start(bf16[4,40,1152]{2,1,0:T(8,128)(2,1)S(1)} %collective-permute-done.18.rest_11_), channel_id=1, source_target_pairs={{0,2},{1,3},{2,0},{3,1},{4,6},{5,7},{6,4},{7,5},{8,10},{9,11},{10,... | collective-permute-start | bytes 1105928 | tf_op jit(solution)/shard_map/ppermute | solution.py:28
where the time goes:
time: 89.6 us; the launch traced here: 89.4 us
  waiting for transfers between devices  40.5 us (45%)
  Pallas kernels  24.5 us (27%)
  starting transfers between devices  18.7 us (21%)
  local copies, waits for them, and re-layouts  4.36 us (5%)
  between operations  0.94 us (1%)
    ppermute x23, waiting for transfers between devices, hop(): return lax.ppermute(block, AXES, route)  40.5 us
    ppermute x23, starting transfers between devices, hop(): return lax.ppermute(block, AXES, route)  18.7 us
    pallas_call x1, Pallas kernels, on_device(): pl.pallas_call(functools.partial(second_kernel, plans), out_shape=(jax.Sh...  16.5 us
    pallas_call x1, Pallas kernels, on_device(): pl.pallas_call(functools.partial(first_kernel, plans[0]), out_shape=tuple...  5.73 us
    unnamed x8, local copies, waits for them, and re-layouts  4.36 us
  transfers between devices with their start and end apart: 23, of which 9 were waited for; matrix products, arithmetic and copies ran while one was open for 0% of the time, Pallas kernels for 7%

commit v1 on v0

--- a/solution.py
+++ b/solution.py
@@ -13,7 +13,8 @@
 LANES = 128
 SUBLANES = 8
 AXES = ("expert", "dp")
-KERNEL_VMEM = 28 * 1024 * 1024
+KERNEL_VMEM = 18 * 1024 * 1024
+PICK_VMEM = 40 * 1024 * 1024
 PIECE = 1280
 
 
@@ -72,7 +73,26 @@
     return jnp.where(mask, 1.0, 0.0).astype(jnp.bfloat16)
 
 
-def pick_kernel(window, folds, group_ref, routes_ref, gates_ref, tokens_ref, cotangent_ref, *outs):
+def pick_kernel(window, folds, group_ref, routes_hbm, gates_hbm, tokens_hbm, cotangent_hbm, *rest):
+    outs = rest[:window]
+    routes_ref, gates_ref, tokens_ref, cotangent_ref, small_sem, sems = rest[window:]
+    small = [
+        pltpu.make_async_copy(routes_hbm, routes_ref, small_sem.at[0]),
+        pltpu.make_async_copy(gates_hbm, gates_ref, small_sem.at[1]),
+    ]
+    copies = []
+    for f in range(folds):
+        where = pl.ds(f * (tokens_ref.shape[1] // folds), tokens_ref.shape[1] // folds)
+        copies.append(
+            [
+                pltpu.make_async_copy(source.at[:, where], target.at[:, where], sems.at[f, i])
+                for i, (source, target) in enumerate(((tokens_hbm, tokens_ref), (cotangent_hbm, cotangent_ref)))
+            ]
+        )
+    for copy in small + [c for pair in copies for c in pair]:
+        copy.start()
+    for copy in small:
+        copy.wait()
     count = tokens_ref.shape[0]
     fold = tokens_ref.shape[1] // folds
     span = 2 * CAP * folds
@@ -100,6 +120,8 @@
         where = pl.ds(f * fold, fold)
         left = jnp.concatenate([one_hot(hit & here) for hit in inputs_at], axis=0)
         right = jnp.concatenate([one_hot(hit & here) for hit in scaled_at], axis=0)
+        for copy in copies[f]:
+            copy.wait()
         total += dot(left, tokens_ref[:, where], ((1,), (0,)))
         total += weight * dot(right, cotangent_ref[:, where], ((1,), (0,)))
     for k, out in enumerate(outs):
@@ -129,10 +151,19 @@
         out[...] = whole[:, low:high]
 
 
+def load_kernel(count, *refs):
+    sems = refs[-1]
+    copies = [pltpu.make_async_copy(refs[i], refs[count + 1 + i], sems.at[i]) for i in range(count)]
+    for copy in copies:
+        copy.start()
+    for copy in copies:
+        copy.wait()
+
+
 class Plan:
     def __init__(self, count, places, edges, half):
         self.count = count
-        self.rows = -(-count // (2 * SUBLANES)) * 2 * SUBLANES
+        self.rows = -(-count // SUBLANES) * SUBLANES
         self.start = 2 * count - self.rows
         self.shift = count - self.start
         self.places = places
@@ -154,37 +185,31 @@
     return [[flat[(lineage * parts + p) * 2 : (lineage * parts + p) * 2 + 2] for p in range(parts)] for lineage in range(2)]
 
 
-def forward(plan, pairs, core, weights, held, sems, pre):
-    gate_held, up_held, down_held = held
-    rows, chips, units = plan.rows, plan.chips, gate_held.shape[1]
-    steps = []
+def add_forward(plan, pairs, halves, core, weights, pre):
+    gate_ref, up_ref, down_ref = weights
+    rows, each = plan.rows, plan.chips // 2
     for lineage in range(2):
+        side = core ^ lineage
         for p, (low, high) in enumerate(plan.edges):
-            side = core ^ lineage
             where = pl.ds(pl.multiple_of(side * plan.half + low, LANES), high - low)
-            spots = [(where, slice(None)), (where, slice(None)), (slice(None), where)]
-            copies = [
-                pltpu.make_async_copy(w.at[at], h.at[at], sems.at[len(steps), i])
-                for i, (w, h, at) in enumerate(zip(weights, held, spots))
-            ]
-            for copy in copies:
-                copy.start()
-            steps.append((lineage, p, low, high, side, where, copies))
-    for lineage, p, low, high, side, where, copies in steps:
-        for copy in copies:
-            copy.wait()
-        inputs = plan.take(pairs[lineage][p], 0, high - low, False)
-        scaled = plan.take(pairs[lineage][p], 0, high - low, True)
-        sums = (
-            dot(inputs, gate_held[where, :], ((1,), (0,))),
-            dot(inputs, up_held[where, :], ((1,), (0,))),
-            dot(scaled, down_held[:, where], ((1,), (1,))),
-        )
-        for place in range(chips):
-            m = plan.chip(side, p, place)
-            for i, value in enumerate(sums):
-                part = value[place * rows : (place + 1) * rows]
-                pre[i, m] = part if lineage + p == 0 else pre[i, m] + part
+            refs = [pairs[lineage][p][h] for h in halves]
+            inputs = plan.take(refs, 0, high - low, False)
+            scaled = plan.take(refs, 0, high - low, True)
+            sums = (
+                dot(inputs, gate_ref[where, :], ((1,), (0,))),
+                dot(inputs, up_ref[where, :], ((1,), (0,))),
+                dot(scaled, down_ref[:, where], ((1,), (1,))),
+            )
+            for j, h in enumerate(halves):
+                for n in range(each):
+                    m = plan.chip(side, p, h * each + n)
+                    at = (j * each + n) * rows
+                    for i, value in enumerate(sums):
+                        pre[i, m] += value[at : at + rows]
+
+
+def finish(plan, pre, delta_ref, hidden_ref):
+    rows, chips, units = plan.rows, plan.chips, hidden_ref.shape[2]
     gate_pre, up_pre, back = [pre[i].reshape(chips * rows, units) for i in range(3)]
     total = chips * rows
     if plan.shift:
@@ -197,71 +222,80 @@
         hidden = pltpu.roll(hidden, plan.shift, 0)
     gate_delta = jnp.where(live, back * up_pre * sigmoid * (1.0 + gate_pre * (1.0 - sigmoid)), 0.0)
     up_delta = jnp.where(live, back * active, 0.0)
-    return [v.astype(jnp.bfloat16).reshape(chips, rows, units) for v in (gate_delta, up_delta, hidden)]
-
-
-def first_kernel(plan, core_ref, gate_ref, up_ref, down_ref, *rest):
-    parts = len(plan.edges)
-    pairs = in_pairs(rest[: 4 * parts], parts)
-    delta_ref, hidden_ref, pre, gate_held, up_held, down_held, sems = rest[4 * parts :]
-    units = gate_held.shape[1]
-    held = (gate_held, up_held, down_held)
-    gate_delta, up_delta, hidden = forward(plan, pairs, core_ref[0], (gate_ref, up_ref, down_ref), held, sems, pre)
-    delta_ref[:, :, :units] = gate_delta
-    delta_ref[:, :, units:] = up_delta
-    hidden_ref[...] = hidden
-
-
-def second_kernel(plans, core_ref, first_delta, first_hidden, gate_ref, up_ref, down_ref, *rest):
+    delta_ref[:, :, :units] = gate_delta.astype(jnp.bfloat16).reshape(chips, rows, units)
+    delta_ref[:, :, units:] = up_delta.astype(jnp.bfloat16).reshape(chips, rows, units)
+    hidden_ref[...] = hidden.astype(jnp.bfloat16).reshape(chips, rows, units)
+
+
+def piece_of(plans):
+    return min(PIECE, max(1, 4096 // sum(plan.chips * plan.rows for plan in plans)) * LANES)
+
+
+def gradients(waves, core):
+    plan = waves[0][0]
+    piece = piece_of([w[0] for w in waves])
+    for lineage in range(2):
+        side = core ^ lineage
+        for p, (begin, end) in enumerate(plan.edges):
+            order = [plan.chip(side, p, place) for place in range(plan.chips)]
+            delta = jnp.concatenate([w[2][m] for w in waves for m in order], axis=0)
+            hidden = jnp.concatenate([w[3][m] for w in waves for m in order], axis=0)
+            for low, high in cut(end - begin, -(-(end - begin) // piece)):
+                inputs = jnp.concatenate([w[0].take(w[1][lineage][p], low, high - low, False) for w in waves], axis=0)
+                scaled = jnp.concatenate([w[0].take(w[1][lineage][p], low, high - low, True) for w in waves], axis=0)
+                tall = dot(inputs, delta, ((0,), (0,)))
+                wide = dot(hidden, scaled, ((0,), (0,)))
+                yield side, begin + low, high - low, tall, wide
+
+
+def first_kernel(plans, core_ref, gate_ref, up_ref, down_ref, *rest):
     first, second = plans
     parts = len(first.edges)
-    first_pairs = in_pairs(rest[: 4 * parts], parts)
-    second_pairs = in_pairs(rest[4 * parts : 8 * parts], parts)
-    gate_out, up_out, down_out, delta_ref, hidden_ref, pre, gate_held, up_held, down_held, sems, tall, wide, tall_sem, wide_sem = rest[8 * parts :]
     core = core_ref[0]
-    chips, units = second.chips, gate_held.shape[1]
-    held = (gate_held, up_held, down_held)
-    gate_delta, up_delta, hidden = forward(second, second_pairs, core, (gate_ref, up_ref, down_ref), held, sems, pre)
-    delta_ref[:, :, :units] = gate_delta
-    delta_ref[:, :, units:] = up_delta
-    hidden_ref[...] = hidden
+    weights = (gate_ref, up_ref, down_ref)
+    pairs = in_pairs(rest[: 4 * parts], parts)
+    rest = rest[4 * parts :]
+    early = [[(rest[lineage * parts + p], None) for p in range(parts)] for lineage in range(2)]
+    delta_ref, hidden_ref, late, pre = rest[2 * parts :]
+    pre[...] = jnp.zeros_like(pre)
+    add_forward(first, pairs, (0, 1), core, weights, pre)
+    finish(first, pre, delta_ref, hidden_ref)
+    late[...] = jnp.zeros_like(late)
+    add_forward(second, early, (0,), core, weights, late)
+
+
+def second_kernel(plans, core_ref, gate_ref, up_ref, down_ref, *rest):
+    first, second = plans
+    parts = len(first.edges)
+    core = core_ref[0]
+    weights = (gate_ref, up_ref, down_ref)
+    units = gate_ref.shape[1]
+    pairs = in_pairs(rest[: 4 * parts], parts)
+    first_pairs = in_pairs(rest[4 * parts : 8 * parts], parts)
+    first_delta, first_hidden, late = rest[8 * parts : 8 * parts + 3]
+    gate_out, up_out, down_out, pre, delta_ref, hidden_ref, tall_held, wide_held, tall_sem, wide_sem = rest[8 * parts + 3 :]
+    pre[...] = late[...]
+    add_forward(second, pairs, (1,), core, weights, pre)
+    waves = [(first, first_pairs, first_delta, first_hidden), (second, pairs, delta_ref, hidden_ref)]
+    finish(second, pre, delta_ref, hidden_ref)
     flying = [[], []]
-    turn = 0
-    for lineage in range(2):
-        side = core ^ lineage
-        for p, (begin, end) in enumerate(first.edges):
-            order = [first.chip(side, p, place) for place in range(chips)]
-            delta = jnp.concatenate([first_delta[m] for m in order] + [delta_ref[m] for m in order], axis=0)
-            hidden = jnp.concatenate([first_hidden[m] for m in order] + [hidden_ref[m] for m in order], axis=0)
-            for low, high in cut(end - begin, -(-(end - begin) // PIECE)):
-                width = high - low
-                where = pl.ds(pl.multiple_of(side * first.half + begin + low, LANES), width)
-                slot = turn % 2
-                turn += 1
-                for copy in flying[slot]:
-                    copy.wait()
-
-                def rows_of(scaled):
-                    return jnp.concatenate(
-                        (
-                            first.take(first_pairs[lineage][p], low, width, scaled),
-                            second.take(second_pairs[lineage][p], low, width, scaled),
-                        ),
-                        axis=0,
-                    )
-
-                both = dot(rows_of(False), delta, ((0,), (0,))).astype(jnp.bfloat16)
-                tall[slot, 0, :width, :] = both[:, :units]
-                tall[slot, 1, :width, :] = both[:, units:]
-                wide[slot, :, :width] = dot(hidden, rows_of(True), ((0,), (0,))).astype(jnp.bfloat16)
-                copies = [
-                    pltpu.make_async_copy(tall.at[slot, 0, pl.ds(0, width), :], gate_out.at[where, :], tall_sem.at[slot, 0]),
-                    pltpu.make_async_copy(tall.at[slot, 1, pl.ds(0, width), :], up_out.at[where, :], tall_sem.at[slot, 1]),
-                    pltpu.make_async_copy(wide.at[slot, :, pl.ds(0, width)], down_out.at[:, where], wide_sem.at[slot]),
-                ]
-                for copy in copies:
-                    copy.start()
-                flying[slot] = copies
+    for turn, (side, low, width, tall, wide) in enumerate(gradients(waves, core)):
+        where = pl.ds(pl.multiple_of(side * second.half + low, LANES), width)
+        slot = turn % 2
+        for copy in flying[slot]:
+            copy.wait()
+        both = tall.astype(jnp.bfloat16)
+        tall_held[slot, 0, :width, :] = both[:, :units]
+        tall_held[slot, 1, :width, :] = both[:, units:]
+        wide_held[slot, :, :width] = wide.astype(jnp.bfloat16)
+        copies = [
+            pltpu.make_async_copy(tall_held.at[slot, 0, pl.ds(0, width), :], gate_out.at[where, :], tall_sem.at[slot, 0]),
+            pltpu.make_async_copy(tall_held.at[slot, 1, pl.ds(0, width), :], up_out.at[where, :], tall_sem.at[slot, 1]),
+            pltpu.make_async_copy(wide_held.at[slot, :, pl.ds(0, width)], down_out.at[:, where], wide_sem.at[slot]),
+        ]
+        for copy in copies:
+            copy.start()
+        flying[slot] = copies
     for copies in flying:
         for copy in copies:
             copy.wait()
@@ -283,6 +317,9 @@
     def near(arrays):
         return [pltpu.with_memory_space_constraint(x, pltpu.VMEM) for x in arrays]
 
+    def far(arrays):
+        return [pltpu.with_memory_space_constraint(x, pltpu.HBM) for x in arrays]
+
     params = pltpu.CompilerParams(vmem_limit_bytes=KERNEL_VMEM)
     folds = 2
     while 2 * CAP * folds % SUBLANES:
@@ -291,11 +328,28 @@
     picked = pl.pallas_call(
         functools.partial(pick_kernel, window, folds),
         out_shape=(jax.ShapeDtypeStruct((span, width // folds), jnp.bfloat16),) * window,
-        in_specs=[smem] + [vmem] * 4,
+        in_specs=[smem] + [hbm] * 4,
         out_specs=(vmem,) * window,
+        scratch_shapes=[
+            pltpu.VMEM(routes.shape[::-1], routes.dtype),
+            pltpu.VMEM(route_gates.shape[::-1], route_gates.dtype),
+            pltpu.VMEM(tokens.shape, tokens.dtype),
+            pltpu.VMEM(cotangent.shape, cotangent.dtype),
+            pltpu.SemaphoreType.DMA((2,)),
+            pltpu.SemaphoreType.DMA((folds, 2)),
+        ],
+        compiler_params=pltpu.CompilerParams(vmem_limit_bytes=PICK_VMEM),
+    )(group, *far((routes.T, route_gates.T, tokens, cotangent)))
+    weights = far((gate_weight[0], up_weight[0], down_weight[0]))
+    weights = pl.pallas_call(
+        functools.partial(load_kernel, len(weights)),
+        out_shape=tuple(jax.ShapeDtypeStruct(w.shape, w.dtype) for w in weights),
+        in_specs=[hbm] * (len(weights) + 1),
+        out_specs=(vmem,) * len(weights),
+        scratch_shapes=[pltpu.SemaphoreType.DMA((len(weights),))],
+        cost_estimate=pl.CostEstimate(flops=1 << 32, bytes_accessed=12 * width * units, transcendentals=0),
         compiler_params=params,
-    )(group, routes.T, route_gates.T, tokens, cotangent)
-    weights = [pltpu.with_memory_space_constraint(w[0], pltpu.HBM) for w in (gate_weight, up_weight, down_weight)]
+    )(*weights, picked[0])
     partner = (1, 0)
     landed = [picked[0]]
     for k in range(1, window):
@@ -339,29 +393,25 @@
 
     chips = plans[0].chips
 
-    def delta_shapes(plan, make):
+    def of_rows(plan, make):
         return [make((chips, plan.rows, 2 * units), jnp.bfloat16), make((chips, plan.rows, units), jnp.bfloat16)]
 
-    def forward_scratch(plan):
-        return [
-            pltpu.VMEM((3, chips, plan.rows, units), jnp.float32),
-            pltpu.VMEM((width, units), jnp.bfloat16),
-            pltpu.VMEM((width, units), jnp.bfloat16),
-            pltpu.VMEM((units, width), jnp.bfloat16),
-            pltpu.SemaphoreType.DMA((2 * len(edges), 3)),
-        ]
+    def sums(plan, make):
+        return make((3, chips, plan.rows, units), jnp.float32)
 
     flops = [6 * chips * plan.rows * width * units for plan in plans]
-    operands[0], _ = lax.optimization_barrier((operands[0], gathered[1][0][0]))
+    held, _ = lax.optimization_barrier((operands[0] + operands[1][::2], gathered[1][0][0]))
+    shapes = of_rows(plans[0], jax.ShapeDtypeStruct) + [sums(plans[1], jax.ShapeDtypeStruct)]
     first = pl.pallas_call(
-        functools.partial(first_kernel, plans[0]),
-        out_shape=tuple(delta_shapes(plans[0], jax.ShapeDtypeStruct)),
-        in_specs=[smem] + [hbm] * 3 + [vmem] * len(operands[0]),
-        out_specs=(vmem, vmem),
-        scratch_shapes=forward_scratch(plans[0]),
-        cost_estimate=pl.CostEstimate(flops=flops[0], bytes_accessed=6 * width * units, transcendentals=0),
+        functools.partial(first_kernel, plans),
+        out_shape=tuple(shapes),
+        in_specs=[smem] + [vmem] * (3 + len(held)),
+        out_specs=(vmem,) * len(shapes),
+        scratch_shapes=[sums(plans[0], pltpu.VMEM)],
+        cost_estimate=pl.CostEstimate(flops=2 * flops[0], bytes_accessed=6 * width * units, transcendentals=0),
         compiler_params=params,
-    )(core, *weights, *near(operands[0]))
+    )(core, *near(weights), *near(held))
+    extra = near(held[: len(operands[0])]) + near(first)
     grads = pl.pallas_call(
         functools.partial(second_kernel, plans),
         out_shape=(
@@ -369,19 +419,19 @@
             jax.ShapeDtypeStruct((width, units), jnp.bfloat16),
             jax.ShapeDtypeStruct((units, width), jnp.bfloat16),
         ),
-        in_specs=[smem] + [vmem] * 2 + [hbm] * 3 + [vmem] * (len(operands[0]) + len(operands[1])),
+        in_specs=[smem] + [vmem] * (3 + len(operands[1]) + len(extra)),
         out_specs=(hbm, hbm, hbm),
-        scratch_shapes=delta_shapes(plans[1], pltpu.VMEM)
-        + forward_scratch(plans[1])
+        scratch_shapes=[sums(plans[1], pltpu.VMEM)]
+        + of_rows(plans[1], pltpu.VMEM)
         + [
-            pltpu.VMEM((2, 2, PIECE, units), jnp.bfloat16),
-            pltpu.VMEM((2, units, PIECE), jnp.bfloat16),
+            pltpu.VMEM((2, 2, piece_of(plans), units), jnp.bfloat16),
+            pltpu.VMEM((2, units, piece_of(plans)), jnp.bfloat16),
             pltpu.SemaphoreType.DMA((2, 2)),
             pltpu.SemaphoreType.DMA((2,)),
         ],
         cost_estimate=pl.CostEstimate(flops=2 * sum(flops), bytes_accessed=12 * width * units, transcendentals=0),
         compiler_params=params,
-    )(core, *near(first), *weights, *near(operands[0]), *near(operands[1]))
+    )(core, *near(weights), *near(operands[1]), *extra)
     return tuple(g[None] for g in grads)
 
 

time: 89.6 us -> 81.6 us (0.911)
  waiting for transfers between devices: 40.5 us -> 33.4 us
  local copies, waits for them, and re-layouts: 4.36 us -> 0 us
  starting transfers between devices: 18.7 us -> 20.8 us
  Pallas kernels: 24.5 us -> 26 us
    ppermute x23, waiting for transfers between devices: 40.5 us -> 33.4 us  [hop(): return lax.ppermute(block, AXES, route)]
    unnamed x8 -> x0, local copies, waits for them, and re-layouts: 4.36 us -> none
    pallas_call x1, Pallas kernels: 16.5 us -> 12.5 us  [on_device(): pl.pallas_call(functools.partial(second_kernel, plans), out_shape=(jax.Sh...]
    pallas_call x1 -> x2, Pallas kernels: 5.73 us -> 8.92 us  [the longest x1 4.69 us: on_device(): pl.pallas_call(functools.partial(first_kernel, plans), out_shape=tuple(sh...]
    pallas_call x1, Pallas kernels: 1.42 us -> 3.74 us  [on_device(): pl.pallas_call(functools.partial(pick_kernel, window, folds), out_shape=(...]
    ppermute x23, starting transfers between devices: 18.7 us -> 20.8 us  [hop(): return lax.ppermute(block, AXES, route)]
  transfers between devices with their start and end apart: 23 -> 23, of which waited for: 9 -> 8; matrix products, arithmetic and copies ran while one was open for 0% -> 0% of each run, Pallas kernels for 7% -> 12%
where the time goes in v1:
time: 81.6 us; the launch traced here: 81.5 us
  waiting for transfers between devices  33.4 us (41%)
  Pallas kernels  26 us (32%)
  starting transfers between devices  20.8 us (25%)
  between operations  0.96 us (1%)
    ppermute x23, waiting for transfers between devices, hop(): return lax.ppermute(block, AXES, route)  33.4 us
    ppermute x23, starting transfers between devices, hop(): return lax.ppermute(block, AXES, route)  20.8 us
    pallas_call x1, Pallas kernels, on_device(): pl.pallas_call(functools.partial(second_kernel, plans), out_shape=(jax.Sh...  12.5 us
    pallas_call x1, Pallas kernels, on_device(): pl.pallas_call(functools.partial(first_kernel, plans), out_shape=tuple(sh...  4.69 us
    pallas_call x1, Pallas kernels, on_device(): pl.pallas_call(functools.partial(load_kernel, len(weights)), out_shape=tu...  4.23 us
    pallas_call x1, Pallas kernels, on_device(): pl.pallas_call(functools.partial(pick_kernel, window, folds), out_shape=(...  3.74 us
  transfers between devices with their start and end apart: 23, of which 8 were waited for; matrix products, arithmetic and copies ran while one was open for 0% of the time, Pallas kernels for 12%

profile of v1, /device:TPU:0, one launch (start us, length us, event | category | flops | bytes accessed | tf_op | source)
XLA Modules:
  0.0 81.5 jit_solution(241745022484230940)
XLA Ops:
  0.6 3.7 %shard_map.94 = (bf16[72,1792]{1,0:T(8,128)(2,1)S(1)}, bf16[72,1792]{1,0:T(8,128)(2,1)S(1)}) custom-call(s32[1]{0:T(128)} %bitcast.4.group_ref, s32[8,128]{1,0:T(8,128)} %bitcast.22, f32[8,128]{1,0:T(8,128)} %bitcast.23, bf16[128,7168]{1,0:T(8,128)(2,1)} %tokens_hbm.1, bf16[128,7168]{1,0:T(8,128)(2,1)} %cotangent_hbm.1), custom_call_target="tpu_custom_call" | custom-call | tf_op jit(solution)/shard_map/pallas_call | solution.py:328
  4.4 0.6 collective-permute-start.2
  5.0 3.6 %collective-permute-start = (bf16[72,1792]{1,0:T(8,128)(2,1)S(1)}, bf16[72,1792]{1,0:T(8,128)(2,1)S(1)}, u32[]{:S(2)}, u32[]{:S(2)}) collective-permute-start(bf16[72,1792]{1,0:T(8,128)(2,1)S(1)} %get-tuple-element.46), channel_id=1, source_target_pairs={{0,16},{1,17},{2,18},{3,19},{4,20},{5,21},{6,22},{7,23},{8,24},{9,... | collective-permute-start | bytes 774152 | tf_op jit(solution)/shard_map/ppermute | solution.py:29
  8.6 0.0 collective-permute-done.2.refs_3_.refs_1_
  8.6 0.3 shard_map.97
  8.9 1.6 %collective-permute-start.14 = (bf16[1,32,1152]{2,1,0:T(8,128)(2,1)S(1)}, bf16[1,32,1152]{2,1,0:T(8,128)(2,1)S(1)}, u32[]{:S(2)}, u32[]{:S(2)}) collective-permute-start(bf16[1,32,1152]{2,1,0:T(8,128)(2,1)S(1)} %bitcast.20), channel_id=1, source_target_pairs={{0,8},{1,9},{2,10},{3,11},{4,12},{5,13},{6,14},{7,15},{8,0},{9,1},... | collective-permute-start | bytes 221192 | tf_op jit(solution)/shard_map/ppermute | solution.py:29
  10.6 1.5 %collective-permute-start.13 = (bf16[1,32,2432]{2,1,0:T(8,128)(2,1)S(1)}, bf16[1,32,2432]{2,1,0:T(8,128)(2,1)S(1)}, u32[]{:S(2)}, u32[]{:S(2)}) collective-permute-start(bf16[1,32,2432]{2,1,0:T(8,128)(2,1)S(1)} %bitcast.16), channel_id=1, source_target_pairs={{0,1},{1,0},{2,6},{3,7},{4,5},{5,4},{6,2},{7,3},{8,9},{9,8},{10,14... | collective-permute-start | bytes 466952 | tf_op jit(solution)/shard_map/ppermute | solution.py:29
  12.0 8.9 %collective-permute-done.refs_0_ = bf16[72,1792]{1,0:T(8,128)(2,1)S(1)} collective-permute-done((bf16[72,1792]{1,0:T(8,128)(2,1)S(1)}, bf16[72,1792]{1,0:T(8,128)(2,1)S(1)}, u32[]{:S(2)}, u32[]{:S(2)}) %collective-permute-start) | collective-permute-done | bytes 258080 | tf_op jit(solution)/shard_map/ppermute | solution.py:29
  20.9 0.0 collective-permute-start.1
  20.9 0.0 collective-permute-done.14
  21.0 0.0 collective-permute-done.13
  21.0 1.6 %collective-permute-start.16 = (bf16[2,32,1152]{2,1,0:T(8,128)(2,1)S(1)}, bf16[2,32,1152]{2,1,0:T(8,128)(2,1)S(1)}, u32[]{:S(2)}, u32[]{:S(2)}) collective-permute-start(bf16[2,32,1152]{2,1,0:T(8,128)(2,1)S(1)} %pad_maximum_fusion.7), channel_id=1, source_target_pairs={{0,4},{1,5},{2,6},{3,7},{4,0},{5,1},{6,2},{7,3},{8,12},{9,13},{10,... | collective-permute-start | bytes 442376 | tf_op jit(solution)/shard_map/ppermute | solution.py:29
  22.7 0.7 collective-permute-start.15
  23.4 0.0 collective-permute-done.1.refs_1_
  23.4 0.5 shard_map.96
  23.9 1.4 %collective-permute-start.4 = (bf16[1,40,1152]{2,1,0:T(8,128)(2,1)S(1)}, bf16[1,40,1152]{2,1,0:T(8,128)(2,1)S(1)}, u32[]{:S(2)}, u32[]{:S(2)}) collective-permute-start(bf16[1,40,1152]{2,1,0:T(8,128)(2,1)S(1)} %bitcast.18), channel_id=1, source_target_pairs={{0,8},{1,9},{2,10},{3,11},{4,12},{5,13},{6,14},{7,15},{8,0},{9,1},... | collective-permute-start | bytes 276488 | tf_op jit(solution)/shard_map/ppermute | solution.py:29
  25.3 1.5 %collective-permute-start.3 = (bf16[1,40,2432]{2,1,0:T(8,128)(2,1)S(1)}, bf16[1,40,2432]{2,1,0:T(8,128)(2,1)S(1)}, u32[]{:S(2)}, u32[]{:S(2)}) collective-permute-start(bf16[1,40,2432]{2,1,0:T(8,128)(2,1)S(1)} %bitcast.14), channel_id=1, source_target_pairs={{0,1},{1,0},{2,6},{3,7},{4,5},{5,4},{6,2},{7,3},{8,9},{9,8},{10,14... | collective-permute-start | bytes 583688 | tf_op jit(solution)/shard_map/ppermute | solution.py:29
  26.8 0.6 collective-permute-done.16
  27.4 4.2 %collective-permute-done.4 = bf16[1,40,1152]{2,1,0:T(8,128)(2,1)S(1)} collective-permute-done((bf16[1,40,1152]{2,1,0:T(8,128)(2,1)S(1)}, bf16[1,40,1152]{2,1,0:T(8,128)(2,1)S(1)}, u32[]{:S(2)}, u32[]{:S(2)}) %collective-permute-start.4) | collective-permute-done | bytes 92192 | tf_op jit(solution)/shard_map/ppermute | solution.py:29
  31.6 0.5 collective-permute-start.6
  32.2 0.8 collective-permute-start.5
  32.9 0.0 collective-permute-done.15
  32.9 0.1 pad_maximum_fusion.1.rest_0_.rest_8_
  33.0 1.6 %collective-permute-start.17 = (bf16[4,32,2432]{2,1,0:T(8,128)(2,1)S(1)}, bf16[4,32,2432]{2,1,0:T(8,128)(2,1)S(1)}, u32[]{:S(2)}, u32[]{:S(2)}) collective-permute-start(bf16[4,32,2432]{2,1,0:T(8,128)(2,1)S(1)} %pad_maximum_fusion.1.rest_0_.rest_8_), channel_id=1, source_target_pairs={{0,4},{1,5},{2,10},{3,11},{4,0},{5,1},{6,14},{7,15},{8,12},{9,13},... | collective-permute-start | bytes 1867784 | tf_op jit(solution)/shard_map/ppermute | solution.py:29
  34.6 2.6 %collective-permute-done.6 = bf16[2,40,1152]{2,1,0:T(8,128)(2,1)S(1)} collective-permute-done((bf16[2,40,1152]{2,1,0:T(8,128)(2,1)S(1)}, bf16[2,40,1152]{2,1,0:T(8,128)(2,1)S(1)}, u32[]{:S(2)}, u32[]{:S(2)}) %collective-permute-start.6) | collective-permute-done | bytes 184352 | tf_op jit(solution)/shard_map/ppermute | solution.py:29
  37.3 6.8 %collective-permute-done.5 = bf16[2,40,2432]{2,1,0:T(8,128)(2,1)S(1)} collective-permute-done((bf16[2,40,2432]{2,1,0:T(8,128)(2,1)S(1)}, bf16[2,40,2432]{2,1,0:T(8,128)(2,1)S(1)}, u32[]{:S(2)}, u32[]{:S(2)}) %collective-permute-start.5) | collective-permute-done | bytes 389152 | tf_op jit(solution)/shard_map/ppermute | solution.py:29
  44.1 0.1 pad_maximum_fusion.rest_8_.rest_0_
  44.1 1.6 %collective-permute-start.7 = (bf16[4,40,2432]{2,1,0:T(8,128)(2,1)S(1)}, bf16[4,40,2432]{2,1,0:T(8,128)(2,1)S(1)}, u32[]{:S(2)}, u32[]{:S(2)}) collective-permute-start(bf16[4,40,2432]{2,1,0:T(8,128)(2,1)S(1)} %pad_maximum_fusion.rest_8_.rest_0_), channel_id=1, source_target_pairs={{0,4},{1,5},{2,10},{3,11},{4,0},{5,1},{6,14},{7,15},{8,12},{9,13},... | collective-permute-start | bytes 2334728 | tf_op jit(solution)/shard_map/ppermute | solution.py:29
  45.8 1.5 %collective-permute-start.8 = (bf16[4,40,1152]{2,1,0:T(8,128)(2,1)S(1)}, bf16[4,40,1152]{2,1,0:T(8,128)(2,1)S(1)}, u32[]{:S(2)}, u32[]{:S(2)}) collective-permute-start(bf16[4,40,1152]{2,1,0:T(8,128)(2,1)S(1)} %pad_maximum_fusion.3.rest_9_.rest_2_), channel_id=1, source_target_pairs={{0,1},{1,0},{2,3},{3,2},{4,5},{5,4},{6,7},{7,6},{8,9},{9,8},{10,11... | collective-permute-start | bytes 1105928 | tf_op jit(solution)/shard_map/ppermute | solution.py:29
  47.3 0.5 collective-permute-start.18
  47.8 8.6 %collective-permute-done.18.rest_3_.rest_11_ = bf16[4,32,1152]{2,1,0:T(8,128)(2,1)S(1)} collective-permute-done((bf16[4,32,1152]{2,1,0:T(8,128)(2,1)S(1)}, bf16[4,32,1152]{2,1,0:T(8,128)(2,1)S(1)}, u32[]{:S(2)}, u32[]{:S(2)}) %collective-permute-start.18) | collective-permute-done | bytes 294944 | tf_op jit(solution)/shard_map/ppermute | solution.py:29
  56.5 0.0 collective-permute-start.21
  56.5 0.5 collective-permute-start.9
  57.0 0.1 collective-permute-start.11
  57.0 0.0 collective-permute-done.7.rest_1_
  57.0 0.4 collective-permute-start.20
  57.5 0.5 collective-permute-done.21.rest_6_.rest_14_
  58.0 0.1 collective-permute-start.10
  58.2 0.0 collective-permute-done.19.rest_4_.rest_12_
  58.2 0.4 collective-permute-start.22
  58.6 1.1 %collective-permute-done.11.rest_11_.rest_6_ = bf16[4,40,1152]{2,1,0:T(8,128)(2,1)S(1)} collective-permute-done((bf16[4,40,1152]{2,1,0:T(8,128)(2,1)S(1)}, bf16[4,40,1152]{2,1,0:T(8,128)(2,1)S(1)}, u32[]{:S(2)}, u32[]{:S(2)}) %collective-permute-start.11) | collective-permute-done | bytes 368672 | tf_op jit(solution)/shard_map/ppermute | solution.py:29
  59.7 0.1 collective-permute-start.12
  59.8 4.2 %shard_map.95 = (bf16[7168,256]{1,0:T(8,128)(2,1)S(1)}, bf16[7168,256]{1,0:T(8,128)(2,1)S(1)}, bf16[256,7168]{1,0:T(8,128)(2,1)S(1)}) custom-call(bf16[7168,256]{1,0:T(8,128)(2,1)} %bitcast.24, bf16[7168,256]{1,0:T(8,128)(2,1)} %bitcast.25, bf16[256,7168]{1,0:T(8,128)(2,1)} %bitcast.26, bf16[72,1792]{1,0:T(8,128)(2,1)S(1)} %get-tuple-element.42.refs_3_.refs_2_.refs_0_), custom_call_target="tpu_custom_call" | custom-call | flops 4294967296 | bytes 22020096 | tf_op jit(solution)/shard_map/pallas_call | solution.py:344
  64.1 0.0 collective-permute-done.9.rest_10_.rest_4_
  64.1 0.0 collective-permute-done.20.rest_5_.rest_13_
  64.1 4.7 %shard_map.98 = (bf16[8,16,512]{2,1,0:T(8,128)(2,1)S(1)}, bf16[8,16,256]{2,1,0:T(8,128)(2,1)S(1)}, f32[3,8,24,256]{3,2,1,0:T(8,128)S(1)}) custom-call(s32[1]{0:T(128)} %bitcast.core_ref, bf16[7168,256]{1,0:T(8,128)(2,1)S(1)} %get-tuple-element.43.gate_ref, bf16[7168,256]{1,0:T(8,128)(2,1)S(1)} %get-tuple-element.44.up_ref, ...), custom_call_target="tpu_custom_call" | custom-call | flops 2818572288 | bytes 11010048 | tf_op jit(solution)/shard_map/pallas_call | solution.py:405
  68.8 0.0 collective-permute-done.12.rest_7_
  68.8 12.5 %shard_map.99 = (bf16[7168,256]{1,0:T(8,128)(2,1)}, bf16[7168,256]{1,0:T(8,128)(2,1)}, bf16[256,7168]{1,0:T(8,128)(2,1)}) custom-call(s32[1]{0:T(128)} %bitcast.core_ref, bf16[7168,256]{1,0:T(8,128)(2,1)S(1)} %get-tuple-element.43.gate_ref, bf16[7168,256]{1,0:T(8,128)(2,1)S(1)} %get-tuple-element.44.up_ref, ...), custom_call_target="tpu_custom_call" | custom-call | flops 7046430720 | bytes 22020096 | tf_op jit(solution)/shard_map/pallas_call | solution.py:415
  (12 shorter events, 0.2 us)
Async XLA Ops:
  4.4 4.2 %collective-permute-start.2 = (bf16[72,1792]{1,0:T(8,128)(2,1)S(1)}, bf16[72,1792]{1,0:T(8,128)(2,1)S(1)}, u32[]{:S(2)}, u32[]{:S(2)}) collective-permute-start(bf16[72,1792]{1,0:T(8,128)(2,1)S(1)} %get-tuple-element.42.refs_3_.refs_2_.refs_0_), channel_id=1, source_target_pairs={{0,2},{1,3},{2,0},{3,1},{4,6},{5,7},{6,4},{7,5},{8,10},{9,11},{10,... | collective-permute-start | bytes 774152 | tf_op jit(solution)/shard_map/ppermute | solution.py:29
  5.0 16.0 %collective-permute-start = (bf16[72,1792]{1,0:T(8,128)(2,1)S(1)}, bf16[72,1792]{1,0:T(8,128)(2,1)S(1)}, u32[]{:S(2)}, u32[]{:S(2)}) collective-permute-start(bf16[72,1792]{1,0:T(8,128)(2,1)S(1)} %get-tuple-element.46), channel_id=1, source_target_pairs={{0,16},{1,17},{2,18},{3,19},{4,20},{5,21},{6,22},{7,23},{8,24},{9,... | collective-permute-start | bytes 774152 | tf_op jit(solution)/shard_map/ppermute | solution.py:29
  8.9 12.0 %collective-permute-start.14 = (bf16[1,32,1152]{2,1,0:T(8,128)(2,1)S(1)}, bf16[1,32,1152]{2,1,0:T(8,128)(2,1)S(1)}, u32[]{:S(2)}, u32[]{:S(2)}) collective-permute-start(bf16[1,32,1152]{2,1,0:T(8,128)(2,1)S(1)} %bitcast.20), channel_id=1, source_target_pairs={{0,8},{1,9},{2,10},{3,11},{4,12},{5,13},{6,14},{7,15},{8,0},{9,1},... | collective-permute-start | bytes 221192 | tf_op jit(solution)/shard_map/ppermute | solution.py:29
  10.6 10.4 %collective-permute-start.13 = (bf16[1,32,2432]{2,1,0:T(8,128)(2,1)S(1)}, bf16[1,32,2432]{2,1,0:T(8,128)(2,1)S(1)}, u32[]{:S(2)}, u32[]{:S(2)}) collective-permute-start(bf16[1,32,2432]{2,1,0:T(8,128)(2,1)S(1)} %bitcast.16), channel_id=1, source_target_pairs={{0,1},{1,0},{2,6},{3,7},{4,5},{5,4},{6,2},{7,3},{8,9},{9,8},{10,14... | collective-permute-start | bytes 466952 | tf_op jit(solution)/shard_map/ppermute | solution.py:29
  20.9 2.5 %collective-permute-start.1 = (bf16[72,1792]{1,0:T(8,128)(2,1)S(1)}, bf16[72,1792]{1,0:T(8,128)(2,1)S(1)}, u32[]{:S(2)}, u32[]{:S(2)}) collective-permute-start(bf16[72,1792]{1,0:T(8,128)(2,1)S(1)} %collective-permute-done.refs_0_), channel_id=1, source_target_pairs={{0,2},{1,3},{2,0},{3,1},{4,6},{5,7},{6,4},{7,5},{8,10},{9,11},{10,... | collective-permute-start | bytes 774152 | tf_op jit(solution)/shard_map/ppermute | solution.py:29
  21.0 6.3 %collective-permute-start.16 = (bf16[2,32,1152]{2,1,0:T(8,128)(2,1)S(1)}, bf16[2,32,1152]{2,1,0:T(8,128)(2,1)S(1)}, u32[]{:S(2)}, u32[]{:S(2)}) collective-permute-start(bf16[2,32,1152]{2,1,0:T(8,128)(2,1)S(1)} %pad_maximum_fusion.7), channel_id=1, source_target_pairs={{0,4},{1,5},{2,6},{3,7},{4,0},{5,1},{6,2},{7,3},{8,12},{9,13},{10,... | collective-permute-start | bytes 442376 | tf_op jit(solution)/shard_map/ppermute | solution.py:29
  22.7 10.3 %collective-permute-start.15 = (bf16[2,32,2432]{2,1,0:T(8,128)(2,1)S(1)}, bf16[2,32,2432]{2,1,0:T(8,128)(2,1)S(1)}, u32[]{:S(2)}, u32[]{:S(2)}) collective-permute-start(bf16[2,32,2432]{2,1,0:T(8,128)(2,1)S(1)} %pad_maximum_fusion.4), channel_id=1, source_target_pairs={{0,8},{1,9},{2,3},{3,2},{4,12},{5,13},{6,7},{7,6},{8,0},{9,1},{10,... | collective-permute-start | bytes 933896 | tf_op jit(solution)/shard_map/ppermute | solution.py:29
  23.9 7.6 %collective-permute-start.4 = (bf16[1,40,1152]{2,1,0:T(8,128)(2,1)S(1)}, bf16[1,40,1152]{2,1,0:T(8,128)(2,1)S(1)}, u32[]{:S(2)}, u32[]{:S(2)}) collective-permute-start(bf16[1,40,1152]{2,1,0:T(8,128)(2,1)S(1)} %bitcast.18), channel_id=1, source_target_pairs={{0,8},{1,9},{2,10},{3,11},{4,12},{5,13},{6,14},{7,15},{8,0},{9,1},... | collective-permute-start | bytes 276488 | tf_op jit(solution)/shard_map/ppermute | solution.py:29
  25.3 6.3 %collective-permute-start.3 = (bf16[1,40,2432]{2,1,0:T(8,128)(2,1)S(1)}, bf16[1,40,2432]{2,1,0:T(8,128)(2,1)S(1)}, u32[]{:S(2)}, u32[]{:S(2)}) collective-permute-start(bf16[1,40,2432]{2,1,0:T(8,128)(2,1)S(1)} %bitcast.14), channel_id=1, source_target_pairs={{0,1},{1,0},{2,6},{3,7},{4,5},{5,4},{6,2},{7,3},{8,9},{9,8},{10,14... | collective-permute-start | bytes 583688 | tf_op jit(solution)/shard_map/ppermute | solution.py:29
  31.6 5.6 %collective-permute-start.6 = (bf16[2,40,1152]{2,1,0:T(8,128)(2,1)S(1)}, bf16[2,40,1152]{2,1,0:T(8,128)(2,1)S(1)}, u32[]{:S(2)}, u32[]{:S(2)}) collective-permute-start(bf16[2,40,1152]{2,1,0:T(8,128)(2,1)S(1)} %pad_maximum_fusion.6), channel_id=1, source_target_pairs={{0,4},{1,5},{2,6},{3,7},{4,0},{5,1},{6,2},{7,3},{8,12},{9,13},{10,... | collective-permute-start | bytes 552968 | tf_op jit(solution)/shard_map/ppermute | solution.py:29
  32.2 11.9 %collective-permute-start.5 = (bf16[2,40,2432]{2,1,0:T(8,128)(2,1)S(1)}, bf16[2,40,2432]{2,1,0:T(8,128)(2,1)S(1)}, u32[]{:S(2)}, u32[]{:S(2)}) collective-permute-start(bf16[2,40,2432]{2,1,0:T(8,128)(2,1)S(1)} %pad_maximum_fusion.2), channel_id=1, source_target_pairs={{0,8},{1,9},{2,3},{3,2},{4,12},{5,13},{6,7},{7,6},{8,0},{9,1},{10,... | collective-permute-start | bytes 1167368 | tf_op jit(solution)/shard_map/ppermute | solution.py:29
  33.0 23.4 %collective-permute-start.17 = (bf16[4,32,2432]{2,1,0:T(8,128)(2,1)S(1)}, bf16[4,32,2432]{2,1,0:T(8,128)(2,1)S(1)}, u32[]{:S(2)}, u32[]{:S(2)}) collective-permute-start(bf16[4,32,2432]{2,1,0:T(8,128)(2,1)S(1)} %pad_maximum_fusion.1.rest_0_.rest_8_), channel_id=1, source_target_pairs={{0,4},{1,5},{2,10},{3,11},{4,0},{5,1},{6,14},{7,15},{8,12},{9,13},... | collective-permute-start | bytes 1867784 | tf_op jit(solution)/shard_map/ppermute | solution.py:29
  44.1 12.9 %collective-permute-start.7 = (bf16[4,40,2432]{2,1,0:T(8,128)(2,1)S(1)}, bf16[4,40,2432]{2,1,0:T(8,128)(2,1)S(1)}, u32[]{:S(2)}, u32[]{:S(2)}) collective-permute-start(bf16[4,40,2432]{2,1,0:T(8,128)(2,1)S(1)} %pad_maximum_fusion.rest_8_.rest_0_), channel_id=1, source_target_pairs={{0,4},{1,5},{2,10},{3,11},{4,0},{5,1},{6,14},{7,15},{8,12},{9,13},... | collective-permute-start | bytes 2334728 | tf_op jit(solution)/shard_map/ppermute | solution.py:29
  45.8 11.2 %collective-permute-start.8 = (bf16[4,40,1152]{2,1,0:T(8,128)(2,1)S(1)}, bf16[4,40,1152]{2,1,0:T(8,128)(2,1)S(1)}, u32[]{:S(2)}, u32[]{:S(2)}) collective-permute-start(bf16[4,40,1152]{2,1,0:T(8,128)(2,1)S(1)} %pad_maximum_fusion.3.rest_9_.rest_2_), channel_id=1, source_target_pairs={{0,1},{1,0},{2,3},{3,2},{4,5},{5,4},{6,7},{7,6},{8,9},{9,8},{10,11... | collective-permute-start | bytes 1105928 | tf_op jit(solution)/shard_map/ppermute | solution.py:29
  47.3 9.2 %collective-permute-start.18 = (bf16[4,32,1152]{2,1,0:T(8,128)(2,1)S(1)}, bf16[4,32,1152]{2,1,0:T(8,128)(2,1)S(1)}, u32[]{:S(2)}, u32[]{:S(2)}) collective-permute-start(bf16[4,32,1152]{2,1,0:T(8,128)(2,1)S(1)} %pad_maximum_fusion.5.rest_2_.rest_10_), channel_id=1, source_target_pairs={{0,1},{1,0},{2,3},{3,2},{4,5},{5,4},{6,7},{7,6},{8,9},{9,8},{10,11... | collective-permute-start | bytes 884744 | tf_op jit(solution)/shard_map/ppermute | solution.py:29
  47.8 10.4 %collective-permute-start.19 = (bf16[4,32,2432]{2,1,0:T(8,128)(2,1)S(1)}, bf16[4,32,2432]{2,1,0:T(8,128)(2,1)S(1)}, u32[]{:S(2)}, u32[]{:S(2)}) collective-permute-start(bf16[4,32,2432]{2,1,0:T(8,128)(2,1)S(1)} %pad_maximum_fusion.1.rest_0_.rest_8_), channel_id=1, source_target_pairs={{0,2},{1,3},{2,0},{3,1},{4,6},{5,7},{6,4},{7,5},{8,10},{9,11},{10,... | collective-permute-start | bytes 1867784 | tf_op jit(solution)/shard_map/ppermute | solution.py:29
  56.5 1.6 %collective-permute-start.21 = (bf16[4,32,1152]{2,1,0:T(8,128)(2,1)S(1)}, bf16[4,32,1152]{2,1,0:T(8,128)(2,1)S(1)}, u32[]{:S(2)}, u32[]{:S(2)}) collective-permute-start(bf16[4,32,1152]{2,1,0:T(8,128)(2,1)S(1)} %pad_maximum_fusion.5.rest_2_.rest_10_), channel_id=1, source_target_pairs={{0,2},{1,3},{2,0},{3,1},{4,6},{5,7},{6,4},{7,5},{8,10},{9,11},{10,... | collective-permute-start | bytes 884744 | tf_op jit(solution)/shard_map/ppermute | solution.py:29
  56.5 7.6 %collective-permute-start.9 = (bf16[4,40,2432]{2,1,0:T(8,128)(2,1)S(1)}, bf16[4,40,2432]{2,1,0:T(8,128)(2,1)S(1)}, u32[]{:S(2)}, u32[]{:S(2)}) collective-permute-start(bf16[4,40,2432]{2,1,0:T(8,128)(2,1)S(1)} %pad_maximum_fusion.rest_8_.rest_0_), channel_id=1, source_target_pairs={{0,2},{1,3},{2,0},{3,1},{4,6},{5,7},{6,4},{7,5},{8,10},{9,11},{10,... | collective-permute-start | bytes 2334728 | tf_op jit(solution)/shard_map/ppermute | solution.py:29
  57.0 2.7 %collective-permute-start.11 = (bf16[4,40,1152]{2,1,0:T(8,128)(2,1)S(1)}, bf16[4,40,1152]{2,1,0:T(8,128)(2,1)S(1)}, u32[]{:S(2)}, u32[]{:S(2)}) collective-permute-start(bf16[4,40,1152]{2,1,0:T(8,128)(2,1)S(1)} %pad_maximum_fusion.3.rest_9_.rest_2_), channel_id=1, source_target_pairs={{0,2},{1,3},{2,0},{3,1},{4,6},{5,7},{6,4},{7,5},{8,10},{9,11},{10,... | collective-permute-start | bytes 1105928 | tf_op jit(solution)/shard_map/ppermute | solution.py:29
  57.0 7.0 %collective-permute-start.20 = (bf16[4,32,2432]{2,1,0:T(8,128)(2,1)S(1)}, bf16[4,32,2432]{2,1,0:T(8,128)(2,1)S(1)}, u32[]{:S(2)}, u32[]{:S(2)}) collective-permute-start(bf16[4,32,2432]{2,1,0:T(8,128)(2,1)S(1)} %collective-permute-done.17.rest_1_.rest_9_), channel_id=1, source_target_pairs={{0,2},{1,3},{2,0},{3,1},{4,6},{5,7},{6,4},{7,5},{8,10},{9,11},{10,... | collective-permute-start | bytes 1867784 | tf_op jit(solution)/shard_map/ppermute | solution.py:29
  58.0 10.8 %collective-permute-start.10 = (bf16[4,40,2432]{2,1,0:T(8,128)(2,1)S(1)}, bf16[4,40,2432]{2,1,0:T(8,128)(2,1)S(1)}, u32[]{:S(2)}, u32[]{:S(2)}) collective-permute-start(bf16[4,40,2432]{2,1,0:T(8,128)(2,1)S(1)} %collective-permute-done.7.rest_1_), channel_id=1, source_target_pairs={{0,2},{1,3},{2,0},{3,1},{4,6},{5,7},{6,4},{7,5},{8,10},{9,11},{10,... | collective-permute-start | bytes 2334728 | tf_op jit(solution)/shard_map/ppermute | solution.py:29
  58.2 5.9 %collective-permute-start.22 = (bf16[4,32,1152]{2,1,0:T(8,128)(2,1)S(1)}, bf16[4,32,1152]{2,1,0:T(8,128)(2,1)S(1)}, u32[]{:S(2)}, u32[]{:S(2)}) collective-permute-start(bf16[4,32,1152]{2,1,0:T(8,128)(2,1)S(1)} %collective-permute-done.18.rest_3_.rest_11_), channel_id=1, source_target_pairs={{0,2},{1,3},{2,0},{3,1},{4,6},{5,7},{6,4},{7,5},{8,10},{9,11},{10,... | collective-permute-start | bytes 884744 | tf_op jit(solution)/shard_map/ppermute | solution.py:29
  59.7 9.1 %collective-permute-start.12 = (bf16[4,40,1152]{2,1,0:T(8,128)(2,1)S(1)}, bf16[4,40,1152]{2,1,0:T(8,128)(2,1)S(1)}, u32[]{:S(2)}, u32[]{:S(2)}) collective-permute-start(bf16[4,40,1152]{2,1,0:T(8,128)(2,1)S(1)} %collective-permute-done.8.rest_3_), channel_id=1, source_target_pairs={{0,2},{1,3},{2,0},{3,1},{4,6},{5,7},{6,4},{7,5},{8,10},{9,11},{10,... | collective-permute-start | bytes 1105928 | tf_op jit(solution)/shard_map/ppermute | solution.py:29
